TPU v7x, 8 devices: a whole 2x2x1 slice. The times are simulated.
8 devices in a mesh: graph: 1 (over z), col: 2 (over y), row: 4 (over x, core).
Axes of the slice: x: 2, y: 2, z: 1, core: 2. Of those that a mesh axis runs over, the one named last changes fastest.
Arguments:
- flow_init: float32 [2048, 2048], P(('graph', 'row'), 'col')
- flow_graph: float32 [2048, 2048], P(('graph', 'row'), 'col')
Outputs:
- output: float32 [2048, 2048], P(('graph', 'row'), 'col')
All inputs are finite; a program needn't handle non-finite values.
Results may differ from a plain program's by a relative error of at most 0.001.
Values are sent between devices in bfloat16 or wider.
A program may use at most 1 GiB of HBM per device.

v0:
```python
import jax
import jax.numpy as jnp
from jax import lax
from jax.sharding import PartitionSpec as P

ITERATIONS = 3


def solution(mesh):
    num_cols = mesh.shape["col"]
    block_spec = P(("graph", "row"), "col")

    def device_step(init_blk, graph_blk):
        mat_order = init_blk.shape[1] * num_cols
        graph_panel = lax.all_gather(graph_blk.astype(jnp.bfloat16), "row", axis=0, tiled=True)
        flow_blk = init_blk
        for _ in range(ITERATIONS):
            row_panel = lax.all_gather(flow_blk.astype(jnp.bfloat16), "col", axis=1, tiled=True)
            expanded = jnp.dot(row_panel, graph_panel, preferred_element_type=jnp.float32)
            inflated = expanded * expanded
            col_sum = lax.psum(jnp.sum(inflated, axis=0), "row")
            flow_blk = inflated * (mat_order / col_sum)
        return flow_blk

    return jax.shard_map(device_step, mesh=mesh, in_specs=(block_spec, block_spec), out_specs=block_spec, check_vma=False)
```

profile of v0, /device:TPU:0, one launch (start us, length us, event | category | flops | bytes accessed | tf_op | source)
XLA Modules:
  0.0 181.6 jit_solution(404964171330161768)
XLA Ops:
  6.5 0.0 all-gather.5.cloned.1.call-start
  6.5 2.9 %convert_element_type.12 = bf16[512,1024]{1,0:T(8,128)(2,1)} convert(f32[512,1024]{1,0:T(8,128)} %param.2) | non-fusion elementwise | flops 524288 | bytes 3145728 | tf_op jit(solution)/shard_map/convert_element_type | solution.py:18
  9.4 0.0 all-gather.5.cloned.1.call-update
  9.4 0.0 all-gather.7.cloned.1.call-start
  9.5 0.0 copy-done
  9.5 1.2 convert_element_type.13
  10.7 0.0 all-gather.7.cloned.1.call-update
  10.7 0.0 all-gather.9.cloned.1.call-start
  10.7 31.8 %all-gather.5.cloned.1.call-done = bf16[512,2048]{1,0:T(8,128)(2,1)} async-done(((bf16[512,1024]{1,0:T(8,128)(2,1)}), bf16[512,2048]{1,0:T(8,128)(2,1)}) %all-gather.5.cloned.1.call-update) | async-done | bytes 2097168 | tf_op jit(solution)/shard_map/all_gather | solution.py:18
  42.6 33.1 %all-gather.7.cloned.1.call-done = bf16[2048,1024]{1,0:T(8,128)(2,1)} async-done(((bf16[512,1024]{1,0:T(8,128)(2,1)}), bf16[2048,1024]{1,0:T(8,128)(2,1)}) %all-gather.7.cloned.1.call-update) | async-done | bytes 4194320 | tf_op jit(solution)/shard_map/all_gather | solution.py:15
  75.6 5.2 %multiply_reduce_fusion.2 = (f32[1024]{0:T(1024)S(1)}, f32[512,1024]{1,0:T(8,128)S(1)}) fusion(bf16[512,2048]{1,0:T(8,128)(2,1)} %all-gather.5.cloned.1.call-done, bf16[2048,1024]{1,0:T(8,128)(2,1)} %all-gather.7.cloned.1.call-done), kind=kOutput, calls=%fused_computation.5 | convolution fusion | flops 2148531200 | bytes 8392704 | tf_op jit(solution)/shard_map/dot_general | solution.py:19
  80.8 5.9 %psum.21 = f32[1024]{0:T(1024)S(1)} all-reduce(f32[1024]{0:T(1024)S(1)} %get-tuple-element.5), channel_id=1, replica_groups=mesh['graph'=1,'col'=2,'row'=4] {'row'}, use_global_device_ids=true, to_apply=%region_1.0 | all-reduce | flops 1024 | bytes 8192 | tf_op jit(solution)/shard_map/psum | solution.py:21
  86.7 1.3 multiply_convert_fusion.1
  88.0 0.0 all-gather.9.cloned.1.call-update
  88.0 0.0 all-gather.11.cloned.1.call-start
  88.0 31.3 %all-gather.9.cloned.1.call-done = bf16[512,2048]{1,0:T(8,128)(2,1)} async-done(((bf16[512,1024]{1,0:T(8,128)(2,1)}), bf16[512,2048]{1,0:T(8,128)(2,1)}) %all-gather.9.cloned.1.call-update) | async-done | bytes 2097168 | tf_op jit(solution)/shard_map/all_gather | solution.py:18
  119.3 5.2 %multiply_reduce_fusion.1 = (f32[1024]{0:T(1024)S(1)}, f32[512,1024]{1,0:T(8,128)S(1)}) fusion(bf16[512,2048]{1,0:T(8,128)(2,1)} %all-gather.9.cloned.1.call-done, bf16[2048,1024]{1,0:T(8,128)(2,1)} %all-gather.7.cloned.1.call-done), kind=kOutput, calls=%fused_computation.4 | convolution fusion | flops 2148531200 | bytes 8392704 | tf_op jit(solution)/shard_map/dot_general | solution.py:19
  124.5 6.3 %psum.22 = f32[1024]{0:T(1024)S(1)} all-reduce(f32[1024]{0:T(1024)S(1)} %get-tuple-element.7), channel_id=1, replica_groups=mesh['graph'=1,'col'=2,'row'=4] {'row'}, use_global_device_ids=true, to_apply=%region_3.0 | all-reduce | flops 1024 | bytes 8192 | tf_op jit(solution)/shard_map/psum | solution.py:21
  130.8 1.3 multiply_convert_fusion
  132.1 0.0 all-gather.11.cloned.1.call-update
  132.1 29.9 %all-gather.11.cloned.1.call-done = bf16[512,2048]{1,0:T(8,128)(2,1)} async-done(((bf16[512,1024]{1,0:T(8,128)(2,1)}), bf16[512,2048]{1,0:T(8,128)(2,1)}) %all-gather.11.cloned.1.call-update) | async-done | bytes 2097168 | tf_op jit(solution)/shard_map/all_gather | solution.py:18
  162.0 5.2 %multiply_reduce_fusion = (f32[1024]{0:T(1024)S(1)}, f32[512,1024]{1,0:T(8,128)S(1)}) fusion(bf16[512,2048]{1,0:T(8,128)(2,1)} %all-gather.11.cloned.1.call-done, bf16[2048,1024]{1,0:T(8,128)(2,1)} %all-gather.7.cloned.1.call-done), kind=kOutput, calls=%fused_computation.3 | convolution fusion | flops 2148531200 | bytes 8392704 | tf_op jit(solution)/shard_map/dot_general | solution.py:19
  167.2 6.3 %psum.23 = f32[1024]{0:T(1024)S(1)} all-reduce(f32[1024]{0:T(1024)S(1)} %get-tuple-element.9), channel_id=1, replica_groups=mesh['graph'=1,'col'=2,'row'=4] {'row'}, use_global_device_ids=true, to_apply=%region_5.0 | all-reduce | flops 1024 | bytes 8192 | tf_op jit(solution)/shard_map/psum | solution.py:21
  173.5 1.6 multiply_multiply_fusion
  (4 shorter events, 0.0 us)
Async XLA Ops:
  6.5 3.0 %copy-start = (f32[512,1024]{1,0:T(8,128)S(1)}, f32[512,1024]{1,0:T(8,128)}, u32[]{:S(2)}) copy-start(f32[512,1024]{1,0:T(8,128)} %param.3) | copy-start | bytes 6291460
  6.5 36.0 %all-gather.5.cloned.1.call-start = ((), (), s32[]{:S(2)}) async-start(), calls=%async_computation | async-start | bytes 3145728 | tf_op jit(solution)/shard_map/all_gather | solution.py:18
  9.4 66.2 %all-gather.7.cloned.1.call-start = ((), (), s32[]{:S(2)}) async-start(), calls=%async_computation.1 | async-start | bytes 5242880 | tf_op jit(solution)/shard_map/all_gather | solution.py:15
  10.7 108.6 %all-gather.9.cloned.1.call-start = ((), (), s32[]{:S(2)}) async-start(), calls=%async_computation.2 | async-start | bytes 3145728 | tf_op jit(solution)/shard_map/all_gather | solution.py:18
  88.0 74.0 %all-gather.11.cloned.1.call-start = ((), (), s32[]{:S(2)}) async-start(), calls=%async_computation.3 | async-start | bytes 3145728 | tf_op jit(solution)/shard_map/all_gather | solution.py:18
Sparse Core Ops, SparseCore 0:
  9.6 32.9 all-gather.4
  44.1 31.4 all-gather.6
  88.1 31.1 all-gather.8
  132.2 29.7 all-gather.10
where the time goes:
time: 182 us
  waiting for transfers between devices  126 us (69%)
  blocking collectives  18.5 us (10%)
  matrix products  15.5 us (9%)
  between operations  13.2 us (7%)
  other arithmetic  8.14 us (4%)
    all_gather x3, waiting for transfers between devices, device_step(): lax.all_gather(flow_blk.astype(jnp.bfloat16), 'col', axis=1, tiled=True)  93.1 us
    all_gather x1, waiting for transfers between devices, device_step(): lax.all_gather(graph_blk.astype(jnp.bfloat16), 'row', axis=0, tiled=True)  33.1 us
    psum x3, blocking collectives, device_step(): col_sum = lax.psum(jnp.sum(inflated, axis=0), 'row')  18.5 us
    dot_general x3, matrix products, device_step(): jnp.dot(row_panel, graph_panel, preferred_element_type=jnp.float32)  15.5 us
    convert_element_type x3, other arithmetic, device_step(): flow_blk.astype(jnp.bfloat16)  5.38 us
  transfers between devices with their start and end apart: 4, of which 4 were waited for; matrix products, arithmetic and copies ran while one was open for 1% of the time, Pallas kernels for 0%

commit v1 on v0

v1 whole, which is shorter than its diff:
```python
import jax
import jax.numpy as jnp
from jax import lax
from jax.experimental import pallas as pl
from jax.experimental.pallas import tpu as pltpu
from jax.sharding import PartitionSpec as P

MESH = pl.DeviceIdType.MESH
BF16 = jnp.bfloat16
F32 = jnp.float32

ROWS = 512
COLS = 1024
ORDER = 2048
SUB = 64
NSUB = ROWS // SUB
KC = 256
NKC = COLS // KC


def mcl_kernel(a_hbm, g_hbm, m_ref, r_ref,
               a_f32, g_f32, G, A0, A1, A2, C1, C2, sums,
               ld_sem, gx_s, gx_r, gy_s, gy_r, dx_s, dx_r, ay_s, ay_r, cf_s, cf_r, ar_s, ar_r):
    graph, col, row = lax.axis_index("graph"), lax.axis_index("col"), lax.axis_index("row")
    x, core = row // 2, row % 2
    nb_x = (graph, col, (1 - x) * 2 + core)
    nb_y = (graph, 1 - col, row)
    nb_c = (graph, col, x * 2 + 1 - core)
    nb_xc = (graph, col, (1 - x) * 2 + 1 - core)

    half_own = lax.rem(x + col, 2)
    half_far = 1 - half_own

    def position(half, side, sub):
        n, s = sub // (128 // SUB), sub % (128 // SUB)
        return pl.multiple_of(half * COLS + KC * n + 128 * side + SUB * s, SUB)

    def remote(ref_src, ref_dst, send, recv, dev):
        return pltpu.make_async_remote_copy(src_ref=ref_src, dst_ref=ref_dst, send_sem=send, recv_sem=recv,
                                            device_id=dev, device_id_type=MESH)

    g_ld = [pltpu.make_async_copy(g_hbm.at[pl.ds(128 * i, 128)], g_f32.at[pl.ds(128 * i, 128)], ld_sem.at[i]) for i in range(4)]
    a_ld = pltpu.make_async_copy(a_hbm, a_f32, ld_sem.at[4])
    for cp in g_ld:
        cp.start()
    a_ld.start()

    barrier = pltpu.get_barrier_semaphore()
    for dev in (nb_x, nb_y, nb_c, nb_xc):
        pl.semaphore_signal(barrier, inc=1, device_id=dev, device_id_type=MESH)

    own_pos = [position(half_own, core, i) for i in range(NSUB)]
    own_at = [G.at[0, pl.ds(own_pos[i], SUB)] for i in range(NSUB)]
    gx_pos = [position(half_far, core, i) for i in range(NSUB)]
    gx_at = [G.at[0, pl.ds(gx_pos[i], SUB)] for i in range(NSUB)]
    gy_at = [G.at[1, pl.ds(own_pos[i], SUB)] for i in range(NSUB)]
    dx_at = [G.at[1, pl.ds(gx_pos[i], SUB)] for i in range(NSUB)]

    gx_cp = [remote(own_at[i], own_at[i], gx_s.at[i], gx_r.at[i], nb_x) for i in range(NSUB)]
    gy_cp = [remote(own_at[i], dx_at[i], gy_s.at[i], gy_r.at[i], nb_y) for i in range(NSUB)]
    dx_cp = [remote(gy_at[i], gy_at[i], dx_s.at[i], dx_r.at[i], nb_x) for i in range(NSUB)]
    cf_cp = [[remote(at[i], at[i], cf_s.at[k, i], cf_r.at[k, i], nb_c) for i in range(NSUB)]
             for k, at in enumerate((own_at, gx_at, gy_at, dx_at))]
    ay_cp = [remote(A0.at[:, pl.ds(KC * n, KC)], A0.at[:, pl.ds(COLS + KC * n, KC)], ay_s.at[n], ay_r.at[n], nb_y)
             for n in range(NKC)]

    def send_own(i):
        gx_cp[i].start()
        gy_cp[i].start()
        cf_cp[0][i].start()

    def put_columns(dst, half, src):
        for c in range(2):
            for n in range(4):
                b = 4 * c + n
                dst[:, half * COLS + KC * n + 128 * c:half * COLS + KC * n + 128 * c + 128] = src(b)

    for i in range(4):
        g_ld[i].wait()
        for s in range(128 // SUB):
            sub = i * (128 // SUB) + s
            G[0, pl.ds(own_pos[sub], SUB), :] = g_f32[SUB * sub:SUB * (sub + 1), :].astype(BF16)
        if i == 0:
            pl.semaphore_wait(barrier, 4)
        else:
            for s in range(128 // SUB):
                send_own((i - 1) * (128 // SUB) + s)
    a_ld.wait()
    put_columns(A0, 0, lambda b: a_f32[:, 128 * b:128 * b + 128].astype(BF16))
    for s in range(128 // SUB):
        send_own(3 * (128 // SUB) + s)

    def dot(a, g):
        return jnp.dot(a, g, preferred_element_type=F32)

    for i in range(NSUB):
        gx_cp[i].wait_recv()
        cf_cp[1][i].start()
        gy_cp[i].wait_recv()
        cf_cp[2][i].start()
        if i >= NSUB - 2:
            dx_cp[i - (NSUB - 2)].start()
            ay_cp[i - (NSUB - 2)].start()
        if i % 2 == 1 and i >= 3:
            n = i // 2 - 1
            for k in (0, 1):
                cf_cp[k][2 * n].wait_recv()
                cf_cp[k][2 * n + 1].wait_recv()
            d = dot(A0[:, KC * n:KC * n + KC], G[0, KC * n:KC * n + KC, :])
            if n == 0:
                C1[:, :COLS] = d
            else:
                C1[:, :COLS] += d
    n = NKC - 1
    for k in (0, 1):
        cf_cp[k][2 * n].wait_recv()
        cf_cp[k][2 * n + 1].wait_recv()
    C1[:, :COLS] += dot(A0[:, KC * n:KC * n + KC], G[0, KC * n:KC * n + KC, :])
    for i in range(NSUB):
        cf_cp[2][i].wait_recv()

    slots = []

    def share(it, lo, width, value, index):
        sums[it, 0, :, lo:lo + width] = value
        cps = []
        for r, dev in ((1, nb_c), (2, nb_x), (3, nb_xc)):
            cp = remote(sums.at[it, 0, :, pl.ds(lo, width)], sums.at[it, r, :, pl.ds(lo, width)],
                        ar_s.at[index, r - 1], ar_r.at[index, r - 1], dev)
            cp.start()
            cps.append(cp)
        slots.extend(cps)
        return it, lo, width, cps

    def gathered(handle):
        it, lo, width, cps = handle
        for cp in cps:
            cp.wait_recv()
        s = [sums[it, r, :, lo:lo + width] for r in range(4)]
        return float(ORDER) / ((s[0] + s[1]) + (s[2] + s[3]))

    def square_and_share(it, dst, lo, width, value, index):
        m = value * value
        dst[:, lo:lo + width] = m
        return share(it, lo, width, jnp.sum(m, axis=0, keepdims=True), index)

    near = None
    for n in range(NKC):
        for s in range(2):
            i = 2 * n + s
            dx_cp[i].wait_recv()
            cf_cp[3][i].start()
            if i + 2 < NSUB:
                dx_cp[i + 2].start()
        ay_cp[n].wait_recv()
        if n + 2 < NKC:
            ay_cp[n + 2].start()
        lo = KC * n
        hi = COLS + lo
        d0 = dot(A0[:, hi:hi + KC], G[0, hi:hi + KC, :])
        if n < NKC - 1:
            C1[:, :COLS] += d0
        else:
            near = square_and_share(0, C1, 0, COLS, C1[:, :COLS] + d0, 0)
        cf_cp[3][2 * n].wait_recv()
        cf_cp[3][2 * n + 1].wait_recv()
        d1 = dot(A0[:, lo:lo + KC], G[1, lo:lo + KC, :]) + dot(A0[:, hi:hi + KC], G[1, hi:hi + KC, :])
        if n == 0:
            C1[:, COLS:] = d1
        elif n < NKC - 1:
            C1[:, COLS:] += d1
        else:
            far = square_and_share(0, C1, COLS, COLS, C1[:, COLS:] + d1, 1)

    f = gathered(near)
    put_columns(A1, 0, lambda b: (C1[:, 128 * b:128 * b + 128] * f[:, 128 * b:128 * b + 128]).astype(BF16))
    for hc in range(2):
        C2[:, hc * COLS:(hc + 1) * COLS] = dot(A1[:, :COLS], G[hc, :COLS, :])
    f2 = gathered(far)
    put_columns(A1, 1, lambda b: (C1[:, COLS + 128 * b:COLS + 128 * b + 128] * f2[:, 128 * b:128 * b + 128]).astype(BF16))
    handles = []
    for hc in range(2):
        lo = hc * COLS
        handles.append(square_and_share(1, C2, lo, COLS, C2[:, lo:lo + COLS] + dot(A1[:, COLS:], G[hc, COLS:, :]), 2 + hc))

    for hc in range(2):
        fh = gathered(handles[hc])
        put_columns(A2, hc, lambda b: (C2[:, hc * COLS + 128 * b:hc * COLS + 128 * b + 128] * fh[:, 128 * b:128 * b + 128]).astype(BF16))
        d = dot(A2[:, hc * COLS:(hc + 1) * COLS], G[0, hc * COLS:(hc + 1) * COLS, :])
        if hc == 0:
            m_ref[...] = d
        else:
            last = square_and_share(2, m_ref, 0, COLS, m_ref[...] + d, 4)
    r_ref[...] = gathered(last)

    for cps in (gx_cp, gy_cp, dx_cp, ay_cp, *cf_cp, slots):
        for cp in cps:
            cp.wait_send()


def solution(mesh):
    block_spec = P(("graph", "row"), "col")

    def device_step(init_blk, graph_blk):
        dma = pltpu.SemaphoreType.DMA
        m, r = pl.pallas_call(
            mcl_kernel,
            name="mcl",
            out_shape=(jax.ShapeDtypeStruct((ROWS, COLS), F32), jax.ShapeDtypeStruct((1, COLS), F32)),
            in_specs=[pl.BlockSpec(memory_space=pl.ANY)] * 2,
            out_specs=(pl.BlockSpec(memory_space=pltpu.VMEM),) * 2,
            scratch_shapes=[
                pltpu.VMEM((ROWS, COLS), F32),
                pltpu.VMEM((ROWS, COLS), F32),
                pltpu.VMEM((2, ORDER, COLS), BF16),
                pltpu.VMEM((ROWS, ORDER), BF16),
                pltpu.VMEM((ROWS, ORDER), BF16),
                pltpu.VMEM((ROWS, ORDER), BF16),
                pltpu.VMEM((ROWS, ORDER), F32),
                pltpu.VMEM((ROWS, ORDER), F32),
                pltpu.VMEM((3, 4, 1, ORDER), F32),
                dma((5,)),
                dma((NSUB,)), dma((NSUB,)),
                dma((NSUB,)), dma((NSUB,)),
                dma((NSUB,)), dma((NSUB,)),
                dma((NKC,)), dma((NKC,)),
                dma((4, NSUB)), dma((4, NSUB)),
                dma((5, 3)), dma((5, 3)),
            ],
            compiler_params=pltpu.CompilerParams(collective_id=0, has_side_effects=True, vmem_limit_bytes=48 * 2**20),
        )(init_blk, graph_blk)
        return m * r

    return jax.shard_map(device_step, mesh=mesh, in_specs=(block_spec, block_spec), out_specs=block_spec, check_vma=False)
```

time: 182 us -> 70 us (0.38)
  waiting for transfers between devices: 126 us -> 0 us
  Pallas kernels: 0 us -> 66.6 us
  blocking collectives: 18.5 us -> 0 us
  matrix products: 15.5 us -> 0 us
  between operations: 13.2 us -> 0.01 us
  other arithmetic: 8.14 us -> 1.68 us
    all_gather x4 -> x0, waiting for transfers between devices: 126 us -> none  [the longest x3 93.1 us: device_step(): lax.all_gather(flow_blk.astype(jnp.bfloat16), 'col', axis=1, tiled=True)]
    pallas_call x0 -> x1, Pallas kernels: none -> 66.6 us  [device_step(): pl.pallas_call(mcl_kernel, name='mcl', out_shape=(jax.ShapeDtypeStruct((R...]
    psum x3 -> x0, blocking collectives: 18.5 us -> none  [device_step(): col_sum = lax.psum(jnp.sum(inflated, axis=0), 'row')]
    dot_general x3 -> x0, matrix products: 15.5 us -> none  [device_step(): jnp.dot(row_panel, graph_panel, preferred_element_type=jnp.float32)]
    convert_element_type x4 -> x0, other arithmetic: 6.55 us -> none  [the longest x3 5.38 us: device_step(): flow_blk.astype(jnp.bfloat16)]
  transfers between devices with their start and end apart: 4 -> 0, of which waited for: 4 -> 0; matrix products, arithmetic and copies ran while one was open for 1% -> 0% of each run, Pallas kernels for 0% -> 0%
where the time goes in v1:
time: 70 us; the launch traced here: 69.9 us
  Pallas kernels  66.6 us (95%)
  other arithmetic  1.68 us (2%)
  local copies, waits for them, and re-layouts  1.59 us (2%)
    pallas_call x1, Pallas kernels, device_step(): pl.pallas_call(mcl_kernel, name='mcl', out_shape=(jax.ShapeDtypeStruct((R...  66.6 us
    mul x1, other arithmetic, device_step(): return m * r  1.68 us
    unnamed x2, local copies, waits for them, and re-layouts  1.59 us

profile of v1, /device:TPU:0, one launch (start us, length us, event | category | flops | bytes accessed | tf_op | source)
XLA Modules:
  0.0 69.9 jit_solution(18389835766281323129)
XLA Ops:
  0.0 0.0 copy-start
  0.0 1.6 %copy-done = f32[512,1024]{1,0:T(8,128)S(1)} copy-done((f32[512,1024]{1,0:T(8,128)S(1)}, f32[512,1024]{1,0:T(8,128)}, u32[]{:S(2)}) %copy-start) | copy-done | bytes 2097176
  1.6 66.6 %mcl.1 = (f32[512,1024]{1,0:T(8,128)S(1)}, f32[1,1024]{1,0:T(1,128)S(1)}) custom-call(f32[512,1024]{1,0:T(8,128)S(1)} %copy-done, f32[512,1024]{1,0:T(8,128)} %g_hbm.1), custom_call_target="tpu_custom_call" | custom-call | tf_op jit(solution)/shard_map/mcl/pallas_call | solution.py:206
  68.2 1.7 %broadcast_multiply_fusion = f32[512,1024]{1,0:T(8,128)} fusion(f32[512,1024]{1,0:T(8,128)S(1)} %get-tuple-element.7, f32[1024]{0:T(1024)S(1)} %bitcast.1), kind=kLoop, calls=%fused_computation | loop fusion | flops 524288 | bytes 4198400 | tf_op jit(solution)/shard_map/mul | solution.py:232
Async XLA Ops:
  0.0 1.6 %copy-start = (f32[512,1024]{1,0:T(8,128)S(1)}, f32[512,1024]{1,0:T(8,128)}, u32[]{:S(2)}) copy-start(f32[512,1024]{1,0:T(8,128)} %a_hbm.1) | copy-start | bytes 6291460

commit v2 on v1

--- a/solution.py
+++ b/solution.py
@@ -16,6 +16,11 @@
 NSUB = ROWS // SUB
 KC = 256
 NKC = COLS // KC
+QW = COLS // 2
+
+
+def place(b):
+    return 2 * (b % 4) + b // 4
 
 
 def mcl_kernel(a_hbm, g_hbm, m_ref, r_ref,
@@ -39,8 +44,8 @@
         return pltpu.make_async_remote_copy(src_ref=ref_src, dst_ref=ref_dst, send_sem=send, recv_sem=recv,
                                             device_id=dev, device_id_type=MESH)
 
-    g_ld = [pltpu.make_async_copy(g_hbm.at[pl.ds(128 * i, 128)], g_f32.at[pl.ds(128 * i, 128)], ld_sem.at[i]) for i in range(4)]
-    a_ld = pltpu.make_async_copy(a_hbm, a_f32, ld_sem.at[4])
+    g_ld = [pltpu.make_async_copy(g_hbm.at[pl.ds(SUB * i, SUB)], g_f32.at[pl.ds(SUB * i, SUB)], ld_sem.at[i]) for i in range(NSUB)]
+    a_ld = pltpu.make_async_copy(a_hbm, a_f32, ld_sem.at[NSUB])
     for cp in g_ld:
         cp.start()
     a_ld.start()
@@ -69,26 +74,20 @@
         gy_cp[i].start()
         cf_cp[0][i].start()
 
-    def put_columns(dst, half, src):
-        for c in range(2):
-            for n in range(4):
-                b = 4 * c + n
-                dst[:, half * COLS + KC * n + 128 * c:half * COLS + KC * n + 128 * c + 128] = src(b)
-
-    for i in range(4):
+    for i in range(NSUB):
         g_ld[i].wait()
-        for s in range(128 // SUB):
-            sub = i * (128 // SUB) + s
-            G[0, pl.ds(own_pos[sub], SUB), :] = g_f32[SUB * sub:SUB * (sub + 1), :].astype(BF16)
+        for b in range(8):
+            p = place(b)
+            G[0, pl.ds(own_pos[i], SUB), 128 * p:128 * p + 128] = g_f32[SUB * i:SUB * (i + 1), 128 * b:128 * b + 128].astype(BF16)
         if i == 0:
             pl.semaphore_wait(barrier, 4)
         else:
-            for s in range(128 // SUB):
-                send_own((i - 1) * (128 // SUB) + s)
+            send_own(i - 1)
     a_ld.wait()
-    put_columns(A0, 0, lambda b: a_f32[:, 128 * b:128 * b + 128].astype(BF16))
-    for s in range(128 // SUB):
-        send_own(3 * (128 // SUB) + s)
+    for b in range(8):
+        p = place(b)
+        A0[:, 128 * p:128 * p + 128] = a_f32[:, 128 * b:128 * b + 128].astype(BF16)
+    send_own(NSUB - 1)
 
     def dot(a, g):
         return jnp.dot(a, g, preferred_element_type=F32)
@@ -121,7 +120,8 @@
 
     slots = []
 
-    def share(it, lo, width, value, index):
+    def share(it, lo, width, value):
+        index = len(slots)
         sums[it, 0, :, lo:lo + width] = value
         cps = []
         for r, dev in ((1, nb_c), (2, nb_x), (3, nb_xc)):
@@ -129,7 +129,7 @@
                         ar_s.at[index, r - 1], ar_r.at[index, r - 1], dev)
             cp.start()
             cps.append(cp)
-        slots.extend(cps)
+        slots.append(cps)
         return it, lo, width, cps
 
     def gathered(handle):
@@ -139,12 +139,16 @@
         s = [sums[it, r, :, lo:lo + width] for r in range(4)]
         return float(ORDER) / ((s[0] + s[1]) + (s[2] + s[3]))
 
-    def square_and_share(it, dst, lo, width, value, index):
+    def square_and_share(it, dst, lo, width, value):
         m = value * value
         dst[:, lo:lo + width] = m
-        return share(it, lo, width, jnp.sum(m, axis=0, keepdims=True), index)
-
-    near = None
+        return share(it, lo, width, jnp.sum(m, axis=0, keepdims=True))
+
+    def rescale(dst, src, q, handle):
+        f = gathered(handle)
+        dst[:, QW * q:QW * (q + 1)] = (src[:, QW * q:QW * (q + 1)] * f).astype(BF16)
+
+    shared = []
     for n in range(NKC):
         for s in range(2):
             i = 2 * n + s
@@ -157,43 +161,56 @@
             ay_cp[n + 2].start()
         lo = KC * n
         hi = COLS + lo
-        d0 = dot(A0[:, hi:hi + KC], G[0, hi:hi + KC, :])
         if n < NKC - 1:
-            C1[:, :COLS] += d0
+            C1[:, :COLS] += dot(A0[:, hi:hi + KC], G[0, hi:hi + KC, :])
         else:
-            near = square_and_share(0, C1, 0, COLS, C1[:, :COLS] + d0, 0)
+            for q in range(2):
+                v = C1[:, QW * q:QW * (q + 1)] + dot(A0[:, hi:hi + KC], G[0, hi:hi + KC, QW * q:QW * (q + 1)])
+                shared.append(square_and_share(0, C1, QW * q, QW, v))
         cf_cp[3][2 * n].wait_recv()
         cf_cp[3][2 * n + 1].wait_recv()
-        d1 = dot(A0[:, lo:lo + KC], G[1, lo:lo + KC, :]) + dot(A0[:, hi:hi + KC], G[1, hi:hi + KC, :])
-        if n == 0:
-            C1[:, COLS:] = d1
-        elif n < NKC - 1:
-            C1[:, COLS:] += d1
+        for q in range(2):
+            c = slice(QW * q, QW * (q + 1))
+            d = dot(A0[:, lo:lo + KC], G[1, lo:lo + KC, c]) + dot(A0[:, hi:hi + KC], G[1, hi:hi + KC, c])
+            at = slice(COLS + QW * q, COLS + QW * (q + 1))
+            if n == 0:
+                C1[:, at] = d
+            elif n < NKC - 1:
+                C1[:, at] += d
+            else:
+                shared.append(square_and_share(0, C1, COLS + QW * q, QW, C1[:, at] + d))
+
+    rescale(A1, C1, 0, shared[0])
+    for hc in range(2):
+        C2[:, hc * COLS:(hc + 1) * COLS] = dot(A1[:, :QW], G[hc, :QW, :])
+    for q in range(1, 4):
+        rescale(A1, C1, q, shared[q])
+    shared = []
+    for q in range(4):
+        c = slice(QW * q, QW * (q + 1))
+        g = slice(QW * (q % 2), QW * (q % 2 + 1))
+        shared.append(square_and_share(1, C2, QW * q, QW, C2[:, c] + dot(A1[:, QW:], G[q // 2, QW:, g])))
+
+    for q in range(4):
+        rescale(A2, C2, q, shared[q])
+        d = dot(A2[:, QW * q:QW * (q + 1)], G[0, QW * q:QW * (q + 1), :])
+        if q == 0:
+            C1[:, :COLS] = d
+        elif q < 3:
+            C1[:, :COLS] += d
         else:
-            far = square_and_share(0, C1, COLS, COLS, C1[:, COLS:] + d1, 1)
-
-    f = gathered(near)
-    put_columns(A1, 0, lambda b: (C1[:, 128 * b:128 * b + 128] * f[:, 128 * b:128 * b + 128]).astype(BF16))
-    for hc in range(2):
-        C2[:, hc * COLS:(hc + 1) * COLS] = dot(A1[:, :COLS], G[hc, :COLS, :])
-    f2 = gathered(far)
-    put_columns(A1, 1, lambda b: (C1[:, COLS + 128 * b:COLS + 128 * b + 128] * f2[:, 128 * b:128 * b + 128]).astype(BF16))
-    handles = []
-    for hc in range(2):
-        lo = hc * COLS
-        handles.append(square_and_share(1, C2, lo, COLS, C2[:, lo:lo + COLS] + dot(A1[:, COLS:], G[hc, COLS:, :]), 2 + hc))
-
-    for hc in range(2):
-        fh = gathered(handles[hc])
-        put_columns(A2, hc, lambda b: (C2[:, hc * COLS + 128 * b:hc * COLS + 128 * b + 128] * fh[:, 128 * b:128 * b + 128]).astype(BF16))
-        d = dot(A2[:, hc * COLS:(hc + 1) * COLS], G[0, hc * COLS:(hc + 1) * COLS, :])
-        if hc == 0:
-            m_ref[...] = d
-        else:
-            last = square_and_share(2, m_ref, 0, COLS, m_ref[...] + d, 4)
-    r_ref[...] = gathered(last)
-
-    for cps in (gx_cp, gy_cp, dx_cp, ay_cp, *cf_cp, slots):
+            v = C1[:, :COLS] + d
+            m = v * v
+            last = share(2, 0, COLS, jnp.sum(m, axis=0, keepdims=True))
+            for b in range(8):
+                p = place(b)
+                m_ref[:, 128 * b:128 * b + 128] = m[:, 128 * p:128 * p + 128]
+    f = gathered(last)
+    for b in range(8):
+        p = place(b)
+        r_ref[:, 128 * b:128 * b + 128] = f[:, 128 * p:128 * p + 128]
+
+    for cps in (gx_cp, gy_cp, dx_cp, ay_cp, *cf_cp, *slots):
         for cp in cps:
             cp.wait_send()
 
@@ -203,11 +220,12 @@
 
     def device_step(init_blk, graph_blk):
         dma = pltpu.SemaphoreType.DMA
+        in_hbm = [pltpu.with_memory_space_constraint(v, pltpu.HBM) for v in (init_blk, graph_blk)]
         m, r = pl.pallas_call(
             mcl_kernel,
             name="mcl",
             out_shape=(jax.ShapeDtypeStruct((ROWS, COLS), F32), jax.ShapeDtypeStruct((1, COLS), F32)),
-            in_specs=[pl.BlockSpec(memory_space=pl.ANY)] * 2,
+            in_specs=[pl.BlockSpec(memory_space=pltpu.HBM)] * 2,
             out_specs=(pl.BlockSpec(memory_space=pltpu.VMEM),) * 2,
             scratch_shapes=[
                 pltpu.VMEM((ROWS, COLS), F32),
@@ -219,16 +237,16 @@
                 pltpu.VMEM((ROWS, ORDER), F32),
                 pltpu.VMEM((ROWS, ORDER), F32),
                 pltpu.VMEM((3, 4, 1, ORDER), F32),
-                dma((5,)),
+                dma((NSUB + 1,)),
                 dma((NSUB,)), dma((NSUB,)),
                 dma((NSUB,)), dma((NSUB,)),
                 dma((NSUB,)), dma((NSUB,)),
                 dma((NKC,)), dma((NKC,)),
                 dma((4, NSUB)), dma((4, NSUB)),
-                dma((5, 3)), dma((5, 3)),
+                dma((9, 3)), dma((9, 3)),
             ],
             compiler_params=pltpu.CompilerParams(collective_id=0, has_side_effects=True, vmem_limit_bytes=48 * 2**20),
-        )(init_blk, graph_blk)
+        )(*in_hbm)
         return m * r
 
     return jax.shard_map(device_step, mesh=mesh, in_specs=(block_spec, block_spec), out_specs=block_spec, check_vma=False)

time: 70 us -> 68.2 us (0.974)
  local copies, waits for them, and re-layouts: 1.59 us -> 0 us
    unnamed x2 -> x0, local copies, waits for them, and re-layouts: 1.59 us -> none
where the time goes in v2:
time: 68.2 us; the launch traced here: 68.1 us
  Pallas kernels  66.4 us (97%)
  other arithmetic  1.68 us (2%)
    pallas_call x1, Pallas kernels, device_step(): pl.pallas_call(mcl_kernel, name='mcl', out_shape=(jax.ShapeDtypeStruct((R...  66.4 us
    mul x1, other arithmetic, device_step(): return m * r  1.68 us

profile of v2, /device:TPU:0, one launch (start us, length us, event | category | flops | bytes accessed | tf_op | source)
XLA Modules:
  0.0 68.1 jit_solution(6061724759457552968)
XLA Ops:
  0.0 66.4 %mcl.1 = (f32[512,1024]{1,0:T(8,128)S(1)}, f32[1,1024]{1,0:T(1,128)S(1)}) custom-call(f32[512,1024]{1,0:T(8,128)} %a_hbm.1, f32[512,1024]{1,0:T(8,128)} %g_hbm.1), custom_call_target="tpu_custom_call" | custom-call | tf_op jit(solution)/shard_map/mcl/pallas_call | solution.py:224
  66.4 1.7 %broadcast_multiply_fusion = f32[512,1024]{1,0:T(8,128)} fusion(f32[512,1024]{1,0:T(8,128)S(1)} %get-tuple-element.7, f32[1024]{0:T(1024)S(1)} %bitcast.1), kind=kLoop, calls=%fused_computation | loop fusion | flops 524288 | bytes 4198400 | tf_op jit(solution)/shard_map/mul | solution.py:250

commit v3 on v2

v3 whole, which is shorter than its diff:
```python
import jax
import jax.numpy as jnp
from jax import lax
from jax.experimental import pallas as pl
from jax.experimental.pallas import tpu as pltpu
from jax.sharding import PartitionSpec as P

MESH = pl.DeviceIdType.MESH
BF16 = jnp.bfloat16
F32 = jnp.float32

ROWS = 512
COLS = 1024
ORDER = 2048
SUB = 128
NSUB = ROWS // SUB
HALF = SUB // 2
TAIL = (NSUB - 1, NSUB - 0.5)
KC = 256
NKC = COLS // KC
PIECES_1 = ((0, 512), (512, 512), (1024, 512), (1536, 512))
PIECES_2 = ((0, 512), (512, 512), (1024, 512), (1536, 512))


def place(b):
    return 2 * (b % 4) + b // 4


def mcl_kernel(a_hbm, g_hbm, m_ref, r_ref,
               a_f32, g_f32, G, A0, A1, A2, C1, C2, sums,
               ld_sem, snd, gx_r, gy_r, dx_r, ay_r, c01_r, c2_r, c3_r, ar_s, ar_r):
    graph, col, row = lax.axis_index("graph"), lax.axis_index("col"), lax.axis_index("row")
    x, core = row // 2, row % 2
    nb_x = (graph, col, (1 - x) * 2 + core)
    nb_y = (graph, 1 - col, row)
    nb_c = (graph, col, x * 2 + 1 - core)
    nb_xc = (graph, col, (1 - x) * 2 + 1 - core)

    half_own = lax.rem(x + col, 2)
    half_far = 1 - half_own

    def position(half, side, sub):
        return pl.multiple_of(half * COLS + KC * (int(sub)) + SUB * side + int(SUB * (sub % 1)), HALF)

    def remote(ref_src, ref_dst, send, recv, dev):
        return pltpu.make_async_remote_copy(src_ref=ref_src, dst_ref=ref_dst, send_sem=send, recv_sem=recv,
                                            device_id=dev, device_id_type=MESH)

    loads = [pltpu.make_async_copy(src, dst, ld_sem.at[i]) for i, (src, dst) in enumerate((
        (g_hbm.at[pl.ds(0, SUB)], g_f32.at[pl.ds(0, SUB)]),
        (g_hbm.at[pl.ds(SUB, ROWS - SUB)], g_f32.at[pl.ds(SUB, ROWS - SUB)]),
        (a_hbm, a_f32)))]
    for cp in loads:
        cp.start()

    barrier = pltpu.get_barrier_semaphore()
    for dev in (nb_x, nb_y, nb_c, nb_xc):
        pl.semaphore_signal(barrier, inc=1, device_id=dev, device_id_type=MESH)

    def rows(hc, half, side, sub, n=SUB):
        return G.at[hc, pl.ds(position(half, side, sub), n)]

    own_at = [rows(0, half_own, core, i) for i in range(NSUB)]
    gx_at = [rows(0, half_far, core, i) for i in range(NSUB)]
    gy_at = [rows(1, half_own, core, i) for i in range(NSUB)]
    dx_at = [rows(1, half_far, core, i) for i in range(NSUB)]
    tail_y = [rows(1, half_own, core, i, HALF) for i in TAIL]
    tail_d = [rows(1, half_far, core, i, HALF) for i in TAIL]

    gx_cp = [remote(own_at[i], own_at[i], snd.at[0], gx_r.at[i], nb_x) for i in range(NSUB)]
    gy_cp = [remote(own_at[i], dx_at[i], snd.at[0], gy_r.at[i], nb_y) for i in range(NSUB)]
    dx_cp = [remote(at, at, snd.at[2], dx_r.at[i], nb_x) for i, at in enumerate(gy_at[:-1] + tail_y)]
    c0_cp = [remote(at, at, snd.at[0], c01_r.at[i], nb_c) for i, at in enumerate(own_at)]
    c1_cp = [remote(at, at, snd.at[1], c01_r.at[i], nb_c) for i, at in enumerate(gx_at)]
    c2_cp = [remote(at, at, snd.at[1], c2_r, nb_c) for at in gy_at]
    c3_cp = [remote(at, at, snd.at[3], c3_r.at[min(i, NSUB - 1)], nb_c) for i, at in enumerate(dx_at[:-1] + tail_d)]
    ay_cp = [remote(A0.at[:, pl.ds(KC * n, KC)], A0.at[:, pl.ds(COLS + KC * n, KC)], snd.at[2], ay_r.at[n], nb_y)
             for n in range(NKC)]

    def bytes_of(count, send, recv):
        at = G.at[0, pl.ds(0, count)] if count <= ORDER else G.at[:, pl.ds(0, count // 2)]
        return remote(at, at, send, recv, nb_c)

    def send_own(i):
        gx_cp[i].start()
        gy_cp[i].start()
        c0_cp[i].start()

    for i in range(NSUB):
        if i < 2:
            loads[i].wait()
        for b in range(8):
            p = place(b)
            G[0, pl.ds(position(half_own, core, i), SUB), 128 * p:128 * p + 128] = (
                g_f32[SUB * i:SUB * (i + 1), 128 * b:128 * b + 128].astype(BF16))
        if i == 0:
            pl.semaphore_wait(barrier, 4)
        else:
            send_own(i - 1)
    loads[2].wait()
    for b in range(8):
        p = place(b)
        A0[:, 128 * p:128 * p + 128] = a_f32[:, 128 * b:128 * b + 128].astype(BF16)
    send_own(NSUB - 1)

    def dot(a, g):
        return jnp.dot(a, g, preferred_element_type=F32)

    def near_step(n):
        bytes_of(2 * SUB, snd.at[0], c01_r.at[n]).wait_recv()
        d = dot(A0[:, KC * n:KC * n + KC], G[0, KC * n:KC * n + KC, :])
        if n == 0:
            C1[:, :COLS] = d
        else:
            C1[:, :COLS] += d

    for i in range(NSUB):
        gx_cp[i].wait_recv()
        c1_cp[i].start()
        gy_cp[i].wait_recv()
        c2_cp[i].start()
        if i == NSUB - 2:
            dx_cp[0].start()
            ay_cp[0].start()
        if i >= 1:
            near_step(i - 1)
    dx_cp[1].start()
    ay_cp[1].start()
    near_step(NSUB - 1)
    bytes_of(ROWS, snd.at[1], c2_r).wait_recv()

    slots = []

    def share(it, lo, width, value):
        index = len(slots)
        slots.append(index)
        sums[it, 0, :, lo:lo + width] = value
        for r, dev in ((1, nb_c), (2, nb_x), (3, nb_xc)):
            remote(sums.at[it, 0, :, pl.ds(lo, width)], sums.at[it, r, :, pl.ds(lo, width)],
                   ar_s.at[it], ar_r.at[index], dev).start()
        return it, lo, width, index

    def three(it, lo, width, index):
        at = sums.at[it, pl.ds(1, 3), :, pl.ds(lo, width)]
        return remote(at, at, ar_s.at[it], ar_r.at[index], nb_c)

    def gathered(handle):
        it, lo, width, index = handle
        three(it, lo, width, index).wait_recv()
        s = [sums[it, r, :, lo:lo + width] for r in range(4)]
        return float(ORDER) / ((s[0] + s[1]) + (s[2] + s[3]))

    def square_and_share(it, dst, lo, width, value):
        m = value * value
        dst[:, lo:lo + width] = m
        return share(it, lo, width, jnp.sum(m, axis=0, keepdims=True))

    def rescale(dst, src, handle):
        f = gathered(handle)
        lo, width = handle[1:3]
        dst[:, lo:lo + width] = (src[:, lo:lo + width] * f).astype(BF16)

    def graph(lo, depth, first, width):
        return G[first // COLS, lo:lo + depth, first % COLS:first % COLS + width]

    shared = []
    for n in range(NKC):
        if n == 0:
            bytes_of(3 * ROWS, snd.at[0], c2_r).wait_send()
        for i in (n,) if n < NSUB - 1 else (n, n + 1):
            dx_cp[i].wait_recv()
            c3_cp[i].start()
            if i + 2 < len(dx_cp):
                dx_cp[i + 2].start()
            if i == n == 2:
                bytes_of(2 * ROWS, snd.at[1], c2_r).wait_send()
        ay_cp[n].wait_recv()
        if n + 2 < NKC:
            ay_cp[n + 2].start()
        lo = KC * n
        hi = COLS + lo
        if n < NKC - 1:
            C1[:, :COLS] += dot(A0[:, hi:hi + KC], G[0, hi:hi + KC, :])
        else:
            for first, width in PIECES_1:
                if first < COLS:
                    v = C1[:, first:first + width] + dot(A0[:, hi:hi + KC], graph(hi, KC, first, width))
                    shared.append(square_and_share(0, C1, first, width, v))
        bytes_of(SUB, snd.at[3], c3_r.at[n]).wait_recv()
        for first, width in PIECES_1:
            if first < COLS:
                continue
            d = dot(A0[:, lo:lo + KC], graph(lo, KC, first, width)) + dot(A0[:, hi:hi + KC], graph(hi, KC, first, width))
            if n == 0:
                C1[:, first:first + width] = d
            elif n < NKC - 1:
                C1[:, first:first + width] += d
            else:
                shared.append(square_and_share(0, C1, first, width, C1[:, first:first + width] + d))

    bytes_of(2 * ROWS, snd.at[2], c2_r).wait_send()
    bytes_of(ROWS, snd.at[3], c2_r).wait_send()
    done = 0
    for t in range(1):
        rescale(A1, C1, shared[t])
        lo, depth = PIECES_1[t]
        for hc in range(2):
            at = slice(hc * COLS, (hc + 1) * COLS)
            d = dot(A1[:, lo:lo + depth], G[hc, lo:lo + depth, :])
            if t == 0:
                C2[:, at] = d
            else:
                C2[:, at] += d
        done = lo + depth
    for handle in shared[1:]:
        rescale(A1, C1, handle)
    three(0, 0, ORDER, 0).wait_send()
    shared = []
    for first, width in PIECES_2:
        v = C2[:, first:first + width] + dot(A1[:, done:], graph(done, ORDER - done, first, width))
        shared.append(square_and_share(1, C2, first, width, v))

    for t, (lo, depth) in enumerate(PIECES_2):
        rescale(A2, C2, shared[t])
        d = dot(A2[:, lo:lo + depth], G[0, lo:lo + depth, :])
        if t == 0:
            C1[:, :COLS] = d
        elif t < len(PIECES_2) - 1:
            C1[:, :COLS] += d
        else:
            v = C1[:, :COLS] + d
            m = v * v
            last = share(2, 0, COLS, jnp.sum(m, axis=0, keepdims=True))
            for b in range(8):
                p = place(b)
                m_ref[:, 128 * b:128 * b + 128] = m[:, 128 * p:128 * p + 128]
    three(1, 0, ORDER, 0).wait_send()
    f = gathered(last)
    for b in range(8):
        p = place(b)
        r_ref[:, 128 * b:128 * b + 128] = f[:, 128 * p:128 * p + 128]
    three(2, 0, COLS, 0).wait_send()


def scale_kernel(m_ref, r_ref, out_hbm, out, sem):
    factor = r_ref[...]
    step = ROWS // 8
    for i in range(8):
        at = pl.ds(step * i, step)
        out[at, :] = m_ref[at, :] * factor
        pltpu.make_async_copy(out.at[at], out_hbm.at[at], sem).start()
    pltpu.make_async_copy(out, out_hbm, sem).wait()


def solution(mesh):
    block_spec = P(("graph", "row"), "col")

    def device_step(init_blk, graph_blk):
        dma = pltpu.SemaphoreType.DMA
        in_hbm = [pltpu.with_memory_space_constraint(v, pltpu.HBM) for v in (init_blk, graph_blk)]
        m, r = pl.pallas_call(
            mcl_kernel,
            name="mcl",
            out_shape=(jax.ShapeDtypeStruct((ROWS, COLS), F32), jax.ShapeDtypeStruct((1, COLS), F32)),
            in_specs=[pl.BlockSpec(memory_space=pltpu.HBM)] * 2,
            out_specs=(pl.BlockSpec(memory_space=pltpu.VMEM),) * 2,
            scratch_shapes=[
                pltpu.VMEM((ROWS, COLS), F32),
                pltpu.VMEM((ROWS, COLS), F32),
                pltpu.VMEM((2, ORDER, COLS), BF16),
                pltpu.VMEM((ROWS, ORDER), BF16),
                pltpu.VMEM((ROWS, ORDER), BF16),
                pltpu.VMEM((ROWS, ORDER), BF16),
                pltpu.VMEM((ROWS, ORDER), F32),
                pltpu.VMEM((ROWS, ORDER), F32),
                pltpu.VMEM((3, 4, 1, ORDER), F32),
                dma((3,)), dma((4,)),
                dma((NSUB,)), dma((NSUB,)), dma((NSUB + 1,)), dma((NKC,)),
                dma((NSUB,)), dma(()), dma((NSUB,)),
                dma((3,)), dma((len(PIECES_1) + len(PIECES_2) + 1,)),
            ],
            compiler_params=pltpu.CompilerParams(collective_id=0, has_side_effects=True, vmem_limit_bytes=48 * 2**20),
        )(*in_hbm)
        return pl.pallas_call(
            scale_kernel,
            name="scale",
            out_shape=jax.ShapeDtypeStruct((ROWS, COLS), F32),
            in_specs=[pl.BlockSpec(memory_space=pltpu.VMEM)] * 2,
            out_specs=pl.BlockSpec(memory_space=pltpu.HBM),
            scratch_shapes=[pltpu.VMEM((ROWS, COLS), F32), dma(())],
            compiler_params=pltpu.CompilerParams(vmem_limit_bytes=8 * 2**20),
        )(m, r)

    return jax.shard_map(device_step, mesh=mesh, in_specs=(block_spec, block_spec), out_specs=block_spec, check_vma=False)
```

time: 68.2 us -> 67.1 us (0.984)
  other arithmetic: 1.68 us -> 0 us
    mul x1 -> x0, other arithmetic: 1.68 us -> none  [device_step(): return m * r]
    pallas_call x0 -> x1, Pallas kernels: none -> 1.33 us  [device_step(): pl.pallas_call(scale_kernel, name='scale', out_shape=jax.ShapeDtypeStruct...]
    pallas_call x1, Pallas kernels: 66.4 us -> 65.7 us  [device_step(): pl.pallas_call(mcl_kernel, name='mcl', out_shape=(jax.ShapeDtypeStruct((R...]
where the time goes in v3:
time: 67.1 us; the launch traced here: 67 us
  Pallas kernels  67 us (100%)
    pallas_call x1, Pallas kernels, device_step(): pl.pallas_call(mcl_kernel, name='mcl', out_shape=(jax.ShapeDtypeStruct((R...  65.7 us

profile of v3, /device:TPU:0, one launch (start us, length us, event | category | flops | bytes accessed | tf_op | source)
XLA Modules:
  0.0 67.0 jit_solution(10525293248356511767)
XLA Ops:
  0.0 65.7 %mcl.1 = (f32[512,1024]{1,0:T(8,128)S(1)}, f32[1,1024]{1,0:T(1,128)S(1)}) custom-call(f32[512,1024]{1,0:T(8,128)} %a_hbm.1, f32[512,1024]{1,0:T(8,128)} %g_hbm.1), custom_call_target="tpu_custom_call" | custom-call | tf_op jit(solution)/shard_map/mcl/pallas_call | solution.py:261
  65.7 1.3 %scale.1 = f32[512,1024]{1,0:T(8,128)} custom-call(f32[512,1024]{1,0:T(8,128)S(1)} %get-tuple-element.7.m_ref, f32[1,1024]{1,0:T(1,128)S(1)} %get-tuple-element.8.r_ref), custom_call_target="tpu_custom_call" | custom-call | tf_op jit(solution)/shard_map/scale/pallas_call | solution.py:284

commit v4 on v3

--- a/solution.py
+++ b/solution.py
@@ -18,8 +18,8 @@
 TAIL = (NSUB - 1, NSUB - 0.5)
 KC = 256
 NKC = COLS // KC
-PIECES_1 = ((0, 512), (512, 512), (1024, 512), (1536, 512))
-PIECES_2 = ((0, 512), (512, 512), (1024, 512), (1536, 512))
+PIECES_1 = ((0, 512), (512, 512), (1024, 1024))
+PIECES_2 = ((1024, 512), (1536, 512), (0, 512), (512, 512))
 
 
 def place(b):
@@ -212,13 +212,23 @@
             else:
                 C2[:, at] += d
         done = lo + depth
-    for handle in shared[1:]:
-        rescale(A1, C1, handle)
+    factors = [gathered(handle) for handle in shared[1:]]
     three(0, 0, ORDER, 0).wait_send()
     shared = []
+    held = None
     for first, width in PIECES_2:
-        v = C2[:, first:first + width] + dot(A1[:, done:], graph(done, ORDER - done, first, width))
-        shared.append(square_and_share(1, C2, first, width, v))
+        v = C2[:, first:first + width]
+        for (lo, depth), f in zip(PIECES_1[1:], factors):
+            if first == PIECES_2[0][0]:
+                A1[:, lo:lo + depth] = (C1[:, lo:lo + depth] * f).astype(BF16)
+            v += dot(A1[:, lo:lo + depth], graph(lo, depth, first, width))
+            if held is not None:
+                shared.append(share(1, *held))
+                held = None
+        m = v * v
+        C2[:, first:first + width] = m
+        held = first, width, jnp.sum(m, axis=0, keepdims=True)
+    shared.append(share(1, *held))
 
     for t, (lo, depth) in enumerate(PIECES_2):
         rescale(A2, C2, shared[t])

time: 67.1 us -> 66.4 us (0.990)
  Pallas kernels: 67 us -> 66.3 us
    pallas_call x1, Pallas kernels: 65.7 us -> 64.9 us  [device_step(): pl.pallas_call(mcl_kernel, name='mcl', out_shape=(jax.ShapeDtypeStruct((R...]
where the time goes in v4:
time: 66.4 us; the launch traced here: 66.3 us
  Pallas kernels  66.3 us (100%)
    pallas_call x1, Pallas kernels, device_step(): pl.pallas_call(mcl_kernel, name='mcl', out_shape=(jax.ShapeDtypeStruct((R...  64.9 us
    pallas_call x1, Pallas kernels, device_step(): pl.pallas_call(scale_kernel, name='scale', out_shape=jax.ShapeDtypeStruct...  1.33 us

profile of v4, /device:TPU:0, one launch (start us, length us, event | category | flops | bytes accessed | tf_op | source)
XLA Modules:
  0.0 66.3 jit_solution(6539933299345048320)
XLA Ops:
  0.0 64.9 %mcl.1 = (f32[512,1024]{1,0:T(8,128)S(1)}, f32[1,1024]{1,0:T(1,128)S(1)}) custom-call(f32[512,1024]{1,0:T(8,128)} %a_hbm.1, f32[512,1024]{1,0:T(8,128)} %g_hbm.1), custom_call_target="tpu_custom_call" | custom-call | tf_op jit(solution)/shard_map/mcl/pallas_call | solution.py:271
  64.9 1.3 %scale.1 = f32[512,1024]{1,0:T(8,128)} custom-call(f32[512,1024]{1,0:T(8,128)S(1)} %get-tuple-element.7.m_ref, f32[1,1024]{1,0:T(1,128)S(1)} %get-tuple-element.8.r_ref), custom_call_target="tpu_custom_call" | custom-call | tf_op jit(solution)/shard_map/scale/pallas_call | solution.py:294

commit v5 on v4

--- a/solution.py
+++ b/solution.py
@@ -15,6 +15,7 @@
 SUB = 128
 NSUB = ROWS // SUB
 HALF = SUB // 2
+LENT = 48
 TAIL = (NSUB - 1, NSUB - 0.5)
 KC = 256
 NKC = COLS // KC
@@ -28,7 +29,7 @@
 
 def mcl_kernel(a_hbm, g_hbm, m_ref, r_ref,
                a_f32, g_f32, G, A0, A1, A2, C1, C2, sums,
-               ld_sem, snd, gx_r, gy_r, dx_r, ay_r, c01_r, c2_r, c3_r, ar_s, ar_r):
+               ld_sem, snd, gx_r, gy_r, dx_r, ay_r, c0_r, c01_r, c2_r, c2x_r, c3_r, ar_s, ar_r):
     graph, col, row = lax.axis_index("graph"), lax.axis_index("col"), lax.axis_index("row")
     x, core = row // 2, row % 2
     nb_x = (graph, col, (1 - x) * 2 + core)
@@ -68,11 +69,21 @@
     tail_d = [rows(1, half_far, core, i, HALF) for i in TAIL]
 
     gx_cp = [remote(own_at[i], own_at[i], snd.at[0], gx_r.at[i], nb_x) for i in range(NSUB)]
-    gy_cp = [remote(own_at[i], dx_at[i], snd.at[0], gy_r.at[i], nb_y) for i in range(NSUB)]
+    def last_rows(hc, half, extra):
+        first = half * COLS + KC * (NSUB - 1)
+        if extra:
+            return G.at[hc, pl.ds(pl.multiple_of(first + 2 * (SUB - LENT), 16), 2 * LENT)]
+        return G.at[hc, pl.ds(pl.multiple_of(first + (SUB - LENT) * core, 16), SUB - LENT)]
+
+    gy_cp = [remote(own_at[i], dx_at[i], snd.at[0], gy_r.at[i], nb_y) for i in range(NSUB - 1)]
+    gy_cp += [remote(last_rows(0, half_own, e), last_rows(1, half_far, e), snd.at[4 if e else 0], gy_r.at[NSUB - 1 + e], nb_y)
+              for e in range(2)]
     dx_cp = [remote(at, at, snd.at[2], dx_r.at[i], nb_x) for i, at in enumerate(gy_at[:-1] + tail_y)]
-    c0_cp = [remote(at, at, snd.at[0], c01_r.at[i], nb_c) for i, at in enumerate(own_at)]
+    c0_cp = [remote(at, at, snd.at[0], c0_r if i == NSUB - 1 else c01_r.at[i], nb_c) for i, at in enumerate(own_at)]
     c1_cp = [remote(at, at, snd.at[1], c01_r.at[i], nb_c) for i, at in enumerate(gx_at)]
-    c2_cp = [remote(at, at, snd.at[1], c2_r, nb_c) for at in gy_at]
+    c2_cp = [remote(at, at, snd.at[1], c2_r, nb_c) for at in gy_at[:-1]]
+    c2_cp += [remote(last_rows(1, half_own, e), last_rows(1, half_own, e), snd.at[4 if e else 1], c2x_r if e else c2_r, nb_c)
+              for e in range(2)]
     c3_cp = [remote(at, at, snd.at[3], c3_r.at[min(i, NSUB - 1)], nb_c) for i, at in enumerate(dx_at[:-1] + tail_d)]
     ay_cp = [remote(A0.at[:, pl.ds(KC * n, KC)], A0.at[:, pl.ds(COLS + KC * n, KC)], snd.at[2], ay_r.at[n], nb_y)
              for n in range(NKC)]
@@ -83,7 +94,8 @@
 
     def send_own(i):
         gx_cp[i].start()
-        gy_cp[i].start()
+        if i < NSUB - 1:
+            gy_cp[i].start()
         c0_cp[i].start()
 
     for i in range(NSUB):
@@ -107,7 +119,7 @@
         return jnp.dot(a, g, preferred_element_type=F32)
 
     def near_step(n):
-        bytes_of(2 * SUB, snd.at[0], c01_r.at[n]).wait_recv()
+        bytes_of((2 if n < NSUB - 1 else 1) * SUB, snd.at[0], c01_r.at[n]).wait_recv()
         d = dot(A0[:, KC * n:KC * n + KC], G[0, KC * n:KC * n + KC, :])
         if n == 0:
             C1[:, :COLS] = d
@@ -119,6 +131,21 @@
         c1_cp[i].start()
         gy_cp[i].wait_recv()
         c2_cp[i].start()
+        if i == 0:
+            c0_cp[-1].wait_recv()
+            gy_cp[NSUB - 1].start()
+
+            @pl.when(core == 1)
+            def _():
+                gy_cp[NSUB].start()
+
+        if i == NSUB - 1:
+
+            @pl.when(core == 1)
+            def _():
+                gy_cp[NSUB].wait_recv()
+                c2_cp[NSUB].start()
+
         if i == NSUB - 2:
             dx_cp[0].start()
             ay_cp[0].start()
@@ -127,7 +154,11 @@
     dx_cp[1].start()
     ay_cp[1].start()
     near_step(NSUB - 1)
-    bytes_of(ROWS, snd.at[1], c2_r).wait_recv()
+    bytes_of(ROWS - LENT, snd.at[1], c2_r).wait_recv()
+
+    @pl.when(core == 0)
+    def _():
+        c2_cp[NSUB].wait_recv()
 
     slots = []
 
@@ -166,14 +197,19 @@
     shared = []
     for n in range(NKC):
         if n == 0:
-            bytes_of(3 * ROWS, snd.at[0], c2_r).wait_send()
+            bytes_of(3 * ROWS - LENT, snd.at[0], c2_r).wait_send()
         for i in (n,) if n < NSUB - 1 else (n, n + 1):
             dx_cp[i].wait_recv()
             c3_cp[i].start()
             if i + 2 < len(dx_cp):
                 dx_cp[i + 2].start()
             if i == n == 2:
-                bytes_of(2 * ROWS, snd.at[1], c2_r).wait_send()
+                bytes_of(2 * ROWS - LENT, snd.at[1], c2_r).wait_send()
+
+                @pl.when(core == 1)
+                def _():
+                    bytes_of(4 * LENT, snd.at[4], c2_r).wait_send()
+
         ay_cp[n].wait_recv()
         if n + 2 < NKC:
             ay_cp[n + 2].start()
@@ -284,9 +320,9 @@
                 pltpu.VMEM((ROWS, ORDER), F32),
                 pltpu.VMEM((ROWS, ORDER), F32),
                 pltpu.VMEM((3, 4, 1, ORDER), F32),
-                dma((3,)), dma((4,)),
-                dma((NSUB,)), dma((NSUB,)), dma((NSUB + 1,)), dma((NKC,)),
-                dma((NSUB,)), dma(()), dma((NSUB,)),
+                dma((3,)), dma((5,)),
+                dma((NSUB,)), dma((NSUB + 1,)), dma((NSUB + 1,)), dma((NKC,)),
+                dma(()), dma((NSUB,)), dma(()), dma(()), dma((NSUB,)),
                 dma((3,)), dma((len(PIECES_1) + len(PIECES_2) + 1,)),
             ],
             compiler_params=pltpu.CompilerParams(collective_id=0, has_side_effects=True, vmem_limit_bytes=48 * 2**20),

time: 66.4 us -> 65.6 us (0.988)
  Pallas kernels: 66.3 us -> 65.5 us
    pallas_call x1, Pallas kernels: 64.9 us -> 64.2 us  [device_step(): pl.pallas_call(mcl_kernel, name='mcl', out_shape=(jax.ShapeDtypeStruct((R...]
where the time goes in v5:
time: 65.6 us; the launch traced here: 65.5 us
  Pallas kernels  65.5 us (100%)
    pallas_call x1, Pallas kernels, device_step(): pl.pallas_call(mcl_kernel, name='mcl', out_shape=(jax.ShapeDtypeStruct((R...  64.2 us
    pallas_call x1, Pallas kernels, device_step(): pl.pallas_call(scale_kernel, name='scale', out_shape=jax.ShapeDtypeStruct...  1.33 us

profile of v5, /device:TPU:0, one launch (start us, length us, event | category | flops | bytes accessed | tf_op | source)
XLA Modules:
  0.0 65.5 jit_solution(634505764338480929)
XLA Ops:
  0.0 64.2 %mcl.1 = (f32[512,1024]{1,0:T(8,128)S(1)}, f32[1,1024]{1,0:T(1,128)S(1)}) custom-call(f32[512,1024]{1,0:T(8,128)} %a_hbm.1, f32[512,1024]{1,0:T(8,128)} %g_hbm.1), custom_call_target="tpu_custom_call" | custom-call | tf_op jit(solution)/shard_map/mcl/pallas_call | solution.py:307
  64.2 1.3 %scale.1 = f32[512,1024]{1,0:T(8,128)} custom-call(f32[512,1024]{1,0:T(8,128)S(1)} %get-tuple-element.7.m_ref, f32[1,1024]{1,0:T(1,128)S(1)} %get-tuple-element.8.r_ref), custom_call_target="tpu_custom_call" | custom-call | tf_op jit(solution)/shard_map/scale/pallas_call | solution.py:330

commit v6 on v5

--- a/solution.py
+++ b/solution.py
@@ -20,6 +20,8 @@
 KC = 256
 NKC = COLS // KC
 PIECES_1 = ((0, 512), (512, 512), (1024, 1024))
+EARLY = 2
+STEP = 512
 PIECES_2 = ((1024, 512), (1536, 512), (0, 512), (512, 512))
 
 
@@ -29,7 +31,7 @@
 
 def mcl_kernel(a_hbm, g_hbm, m_ref, r_ref,
                a_f32, g_f32, G, A0, A1, A2, C1, C2, sums,
-               ld_sem, snd, gx_r, gy_r, dx_r, ay_r, c0_r, c01_r, c2_r, c2x_r, c3_r, ar_s, ar_r):
+               ld_sem, snd, in_r, far_r, c0_r, c01_r, c2_r, c2x_r, c3_r, ar_s, ar_r):
     graph, col, row = lax.axis_index("graph"), lax.axis_index("col"), lax.axis_index("row")
     x, core = row // 2, row % 2
     nb_x = (graph, col, (1 - x) * 2 + core)
@@ -68,24 +70,24 @@
     tail_y = [rows(1, half_own, core, i, HALF) for i in TAIL]
     tail_d = [rows(1, half_far, core, i, HALF) for i in TAIL]
 
-    gx_cp = [remote(own_at[i], own_at[i], snd.at[0], gx_r.at[i], nb_x) for i in range(NSUB)]
+    gx_cp = [remote(own_at[i], own_at[i], snd.at[0], in_r.at[i // 2], nb_x) for i in range(NSUB)]
     def last_rows(hc, half, extra):
         first = half * COLS + KC * (NSUB - 1)
         if extra:
             return G.at[hc, pl.ds(pl.multiple_of(first + 2 * (SUB - LENT), 16), 2 * LENT)]
         return G.at[hc, pl.ds(pl.multiple_of(first + (SUB - LENT) * core, 16), SUB - LENT)]
 
-    gy_cp = [remote(own_at[i], dx_at[i], snd.at[0], gy_r.at[i], nb_y) for i in range(NSUB - 1)]
-    gy_cp += [remote(last_rows(0, half_own, e), last_rows(1, half_far, e), snd.at[4 if e else 0], gy_r.at[NSUB - 1 + e], nb_y)
+    gy_cp = [remote(own_at[i], dx_at[i], snd.at[0], in_r.at[i // 2], nb_y) for i in range(NSUB - 1)]
+    gy_cp += [remote(last_rows(0, half_own, e), last_rows(1, half_far, e), snd.at[3 if e else 0], in_r.at[1 + e], nb_y)
               for e in range(2)]
-    dx_cp = [remote(at, at, snd.at[2], dx_r.at[i], nb_x) for i, at in enumerate(gy_at[:-1] + tail_y)]
-    c0_cp = [remote(at, at, snd.at[0], c0_r if i == NSUB - 1 else c01_r.at[i], nb_c) for i, at in enumerate(own_at)]
-    c1_cp = [remote(at, at, snd.at[1], c01_r.at[i], nb_c) for i, at in enumerate(gx_at)]
+    dx_cp = [remote(at, at, snd.at[2], far_r.at[i], nb_x) for i, at in enumerate(gy_at[:-1] + tail_y)]
+    c0_cp = [remote(at, at, snd.at[0], c0_r if i == NSUB - 1 else c01_r, nb_c) for i, at in enumerate(own_at)]
+    c1_cp = [remote(at, at, snd.at[1], c01_r, nb_c) for at in gx_at]
     c2_cp = [remote(at, at, snd.at[1], c2_r, nb_c) for at in gy_at[:-1]]
-    c2_cp += [remote(last_rows(1, half_own, e), last_rows(1, half_own, e), snd.at[4 if e else 1], c2x_r if e else c2_r, nb_c)
+    c2_cp += [remote(last_rows(1, half_own, e), last_rows(1, half_own, e), snd.at[3 if e else 1], c2x_r if e else c2_r, nb_c)
               for e in range(2)]
-    c3_cp = [remote(at, at, snd.at[3], c3_r.at[min(i, NSUB - 1)], nb_c) for i, at in enumerate(dx_at[:-1] + tail_d)]
-    ay_cp = [remote(A0.at[:, pl.ds(KC * n, KC)], A0.at[:, pl.ds(COLS + KC * n, KC)], snd.at[2], ay_r.at[n], nb_y)
+    c3_cp = [remote(at, at, snd.at[0], c3_r.at[min(i, NSUB - 1)], nb_c) for i, at in enumerate(dx_at[:-1] + tail_d)]
+    ay_cp = [remote(A0.at[:, pl.ds(KC * n, KC)], A0.at[:, pl.ds(COLS + KC * n, KC)], snd.at[2], far_r.at[n if n < NKC - 1 else NSUB + 1], nb_y)
              for n in range(NKC)]
 
     def bytes_of(count, send, recv):
@@ -118,42 +120,30 @@
     def dot(a, g):
         return jnp.dot(a, g, preferred_element_type=F32)
 
-    def near_step(n):
-        bytes_of((2 if n < NSUB - 1 else 1) * SUB, snd.at[0], c01_r.at[n]).wait_recv()
-        d = dot(A0[:, KC * n:KC * n + KC], G[0, KC * n:KC * n + KC, :])
-        if n == 0:
-            C1[:, :COLS] = d
-        else:
-            C1[:, :COLS] += d
-
-    for i in range(NSUB):
-        gx_cp[i].wait_recv()
-        c1_cp[i].start()
-        gy_cp[i].wait_recv()
-        c2_cp[i].start()
-        if i == 0:
-            c0_cp[-1].wait_recv()
-            gy_cp[NSUB - 1].start()
-
-            @pl.when(core == 1)
-            def _():
-                gy_cp[NSUB].start()
-
-        if i == NSUB - 1:
-
-            @pl.when(core == 1)
-            def _():
-                gy_cp[NSUB].wait_recv()
-                c2_cp[NSUB].start()
-
-        if i == NSUB - 2:
-            dx_cp[0].start()
-            ay_cp[0].start()
-        if i >= 1:
-            near_step(i - 1)
-    dx_cp[1].start()
-    ay_cp[1].start()
-    near_step(NSUB - 1)
+    c0_cp[-1].wait_recv()
+    gy_cp[NSUB - 1].start()
+
+    @pl.when(core == 1)
+    def _():
+        gy_cp[NSUB].start()
+
+    for half in range(2):
+        bytes_of(4 * SUB - half * LENT, snd.at[0], in_r.at[half]).wait_recv()
+        for i in (2 * half, 2 * half + 1):
+            c1_cp[i].start()
+            c2_cp[i].start()
+        if half == 0:
+            for i in range(2):
+                dx_cp[i].start()
+                ay_cp[i].start()
+
+    @pl.when(core == 1)
+    def _():
+        gy_cp[NSUB].wait_recv()
+        c2_cp[NSUB].start()
+
+    bytes_of(7 * SUB, snd.at[0], c01_r).wait_recv()
+    C1[:, :COLS] = dot(A0[:, :COLS], G[0, :COLS, :])
     bytes_of(ROWS - LENT, snd.at[1], c2_r).wait_recv()
 
     @pl.when(core == 0)
@@ -168,12 +158,12 @@
         sums[it, 0, :, lo:lo + width] = value
         for r, dev in ((1, nb_c), (2, nb_x), (3, nb_xc)):
             remote(sums.at[it, 0, :, pl.ds(lo, width)], sums.at[it, r, :, pl.ds(lo, width)],
-                   ar_s.at[it], ar_r.at[index], dev).start()
+                   ar_s, ar_r.at[index], dev).start()
         return it, lo, width, index
 
     def three(it, lo, width, index):
         at = sums.at[it, pl.ds(1, 3), :, pl.ds(lo, width)]
-        return remote(at, at, ar_s.at[it], ar_r.at[index], nb_c)
+        return remote(at, at, ar_s, ar_r.at[index], nb_c)
 
     def gathered(handle):
         it, lo, width, index = handle
@@ -194,25 +184,36 @@
     def graph(lo, depth, first, width):
         return G[first // COLS, lo:lo + depth, first % COLS:first % COLS + width]
 
+    def far_piece(i):
+        dx_cp[i].wait_recv()
+        c3_cp[i].start()
+
+    bytes_of(3 * ROWS - LENT, snd.at[0], c2_r).wait_send()
     shared = []
     for n in range(NKC):
-        if n == 0:
-            bytes_of(3 * ROWS - LENT, snd.at[0], c2_r).wait_send()
-        for i in (n,) if n < NSUB - 1 else (n, n + 1):
-            dx_cp[i].wait_recv()
-            c3_cp[i].start()
-            if i + 2 < len(dx_cp):
-                dx_cp[i + 2].start()
-            if i == n == 2:
-                bytes_of(2 * ROWS - LENT, snd.at[1], c2_r).wait_send()
-
-                @pl.when(core == 1)
-                def _():
-                    bytes_of(4 * LENT, snd.at[4], c2_r).wait_send()
-
-        ay_cp[n].wait_recv()
+        if n < NKC - 1:
+            bytes_of(2 * SUB, snd.at[0], far_r.at[n]).wait_recv()
+            c3_cp[n].start()
+        else:
+            far_piece(n)
+        for i in ((2,), (3, 4), (), ())[n]:
+            dx_cp[i].start()
         if n + 2 < NKC:
             ay_cp[n + 2].start()
+        if n == 2:
+            bytes_of(2 * ROWS - LENT, snd.at[1], c2_r).wait_send()
+
+            @pl.when(core == 1)
+            def _():
+                bytes_of(4 * LENT, snd.at[3], c2_r).wait_send()
+
+        if n == NKC - 1:
+
+            @pl.when(core == 1)
+            def _():
+                far_piece(NSUB)
+
+            ay_cp[n].wait_recv()
         lo = KC * n
         hi = COLS + lo
         if n < NKC - 1:
@@ -222,7 +223,13 @@
                 if first < COLS:
                     v = C1[:, first:first + width] + dot(A0[:, hi:hi + KC], graph(hi, KC, first, width))
                     shared.append(square_and_share(0, C1, first, width, v))
-        bytes_of(SUB, snd.at[3], c3_r.at[n]).wait_recv()
+                    if len(shared) == 1:
+
+                        @pl.when(core == 0)
+                        def _():
+                            far_piece(NSUB)
+
+        bytes_of(SUB, snd.at[0], c3_r.at[n]).wait_recv()
         for first, width in PIECES_1:
             if first < COLS:
                 continue
@@ -235,7 +242,7 @@
                 shared.append(square_and_share(0, C1, first, width, C1[:, first:first + width] + d))
 
     bytes_of(2 * ROWS, snd.at[2], c2_r).wait_send()
-    bytes_of(ROWS, snd.at[3], c2_r).wait_send()
+    bytes_of(ROWS, snd.at[0], c2_r).wait_send()
     done = 0
     for t in range(1):
         rescale(A1, C1, shared[t])
@@ -248,19 +255,24 @@
             else:
                 C2[:, at] += d
         done = lo + depth
-    factors = [gathered(handle) for handle in shared[1:]]
+    rescale(A1, C1, shared[1])
+    lo, depth = PIECES_1[1]
+    for first, width in PIECES_2[:EARLY]:
+        C2[:, first:first + width] += dot(A1[:, lo:lo + depth], graph(lo, depth, first, width))
+    f = gathered(shared[2])
     three(0, 0, ORDER, 0).wait_send()
     shared = []
     held = None
-    for first, width in PIECES_2:
+    for t, (first, width) in enumerate(PIECES_2):
         v = C2[:, first:first + width]
-        for (lo, depth), f in zip(PIECES_1[1:], factors):
-            if first == PIECES_2[0][0]:
-                A1[:, lo:lo + depth] = (C1[:, lo:lo + depth] * f).astype(BF16)
-            v += dot(A1[:, lo:lo + depth], graph(lo, depth, first, width))
-            if held is not None:
-                shared.append(share(1, *held))
-                held = None
+        for lo, depth in PIECES_1[2 if t < EARLY else 1:]:
+            for at in range(lo, lo + depth, STEP):
+                if t == 0:
+                    A1[:, at:at + STEP] = (C1[:, at:at + STEP] * f[:, at - lo:at - lo + STEP]).astype(BF16)
+                v += dot(A1[:, at:at + STEP], graph(at, STEP, first, width))
+                if held is not None:
+                    shared.append(share(1, *held))
+                    held = None
         m = v * v
         C2[:, first:first + width] = m
         held = first, width, jnp.sum(m, axis=0, keepdims=True)
@@ -268,6 +280,8 @@
 
     for t, (lo, depth) in enumerate(PIECES_2):
         rescale(A2, C2, shared[t])
+        if t == len(PIECES_2) - 1:
+            three(1, 0, ORDER, 0).wait_send()
         d = dot(A2[:, lo:lo + depth], G[0, lo:lo + depth, :])
         if t == 0:
             C1[:, :COLS] = d
@@ -280,7 +294,6 @@
             for b in range(8):
                 p = place(b)
                 m_ref[:, 128 * b:128 * b + 128] = m[:, 128 * p:128 * p + 128]
-    three(1, 0, ORDER, 0).wait_send()
     f = gathered(last)
     for b in range(8):
         p = place(b)
@@ -320,10 +333,9 @@
                 pltpu.VMEM((ROWS, ORDER), F32),
                 pltpu.VMEM((ROWS, ORDER), F32),
                 pltpu.VMEM((3, 4, 1, ORDER), F32),
-                dma((3,)), dma((5,)),
-                dma((NSUB,)), dma((NSUB + 1,)), dma((NSUB + 1,)), dma((NKC,)),
-                dma(()), dma((NSUB,)), dma(()), dma(()), dma((NSUB,)),
-                dma((3,)), dma((len(PIECES_1) + len(PIECES_2) + 1,)),
+                dma((3,)), dma((4,)), dma((3,)), dma((NSUB + 2,)),
+                dma(()), dma(()), dma(()), dma(()), dma((NSUB,)),
+                dma(()), dma((len(PIECES_1) + len(PIECES_2) + 1,)),
             ],
             compiler_params=pltpu.CompilerParams(collective_id=0, has_side_effects=True, vmem_limit_bytes=48 * 2**20),
         )(*in_hbm)

time: 65.6 us -> 65.5 us (level)
  no operation moved by 1% of the time
where the time goes in v6:
time: 65.5 us; the launch traced here: 65.4 us
  Pallas kernels  65.4 us (100%)
    pallas_call x1, Pallas kernels, device_step(): pl.pallas_call(mcl_kernel, name='mcl', out_shape=(jax.ShapeDtypeStruct((R...  64.1 us
    pallas_call x1, Pallas kernels, device_step(): pl.pallas_call(scale_kernel, name='scale', out_shape=jax.ShapeDtypeStruct...  1.33 us

profile of v6, /device:TPU:0, one launch (start us, length us, event | category | flops | bytes accessed | tf_op | source)
XLA Modules:
  0.0 65.4 jit_solution(9084046312996289738)
XLA Ops:
  0.0 64.1 %mcl.1 = (f32[512,1024]{1,0:T(8,128)S(1)}, f32[1,1024]{1,0:T(1,128)S(1)}) custom-call(f32[512,1024]{1,0:T(8,128)} %a_hbm.1, f32[512,1024]{1,0:T(8,128)} %g_hbm.1), custom_call_target="tpu_custom_call" | custom-call | tf_op jit(solution)/shard_map/mcl/pallas_call | solution.py:320
  64.1 1.3 %scale.1 = f32[512,1024]{1,0:T(8,128)} custom-call(f32[512,1024]{1,0:T(8,128)S(1)} %get-tuple-element.7.m_ref, f32[1,1024]{1,0:T(1,128)S(1)} %get-tuple-element.8.r_ref), custom_call_target="tpu_custom_call" | custom-call | tf_op jit(solution)/shard_map/scale/pallas_call | solution.py:342

commit v7 on v6

--- a/solution.py
+++ b/solution.py
@@ -15,6 +15,7 @@
 SUB = 128
 NSUB = ROWS // SUB
 HALF = SUB // 2
+FIRST = 32
 LENT = 48
 TAIL = (NSUB - 1, NSUB - 0.5)
 KC = 256
@@ -49,10 +50,10 @@
         return pltpu.make_async_remote_copy(src_ref=ref_src, dst_ref=ref_dst, send_sem=send, recv_sem=recv,
                                             device_id=dev, device_id_type=MESH)
 
-    loads = [pltpu.make_async_copy(src, dst, ld_sem.at[i]) for i, (src, dst) in enumerate((
-        (g_hbm.at[pl.ds(0, SUB)], g_f32.at[pl.ds(0, SUB)]),
-        (g_hbm.at[pl.ds(SUB, ROWS - SUB)], g_f32.at[pl.ds(SUB, ROWS - SUB)]),
-        (a_hbm, a_f32)))]
+    cuts = (0, FIRST, 2 * FIRST, SUB, 2 * SUB, ROWS)
+    loads = [pltpu.make_async_copy(g_hbm.at[pl.ds(lo, hi - lo)], g_f32.at[pl.ds(lo, hi - lo)], ld_sem.at[i])
+             for i, (lo, hi) in enumerate(zip(cuts, cuts[1:]))]
+    loads.append(pltpu.make_async_copy(a_hbm, a_f32, ld_sem.at[len(loads)]))
     for cp in loads:
         cp.start()
 
@@ -94,28 +95,37 @@
         at = G.at[0, pl.ds(0, count)] if count <= ORDER else G.at[:, pl.ds(0, count // 2)]
         return remote(at, at, send, recv, nb_c)
 
-    def send_own(i):
-        gx_cp[i].start()
-        if i < NSUB - 1:
-            gy_cp[i].start()
-        c0_cp[i].start()
-
-    for i in range(NSUB):
-        if i < 2:
-            loads[i].wait()
+    def send_own(lo, hi):
+        i = lo // SUB
+        if hi - lo == SUB:
+            gx_cp[i].start()
+            if i < NSUB - 1:
+                gy_cp[i].start()
+            c0_cp[i].start()
+        else:
+            at = G.at[0, pl.ds(pl.multiple_of(position(half_own, core, 0) + lo, FIRST), hi - lo)]
+            there = G.at[1, pl.ds(pl.multiple_of(position(half_far, core, 0) + lo, FIRST), hi - lo)]
+            remote(at, at, snd.at[0], in_r.at[0], nb_x).start()
+            remote(at, there, snd.at[0], in_r.at[0], nb_y).start()
+            remote(at, at, snd.at[0], c01_r, nb_c).start()
+
+    parts = (*zip(cuts, cuts[1:4]), *((SUB * i, SUB * (i + 1)) for i in range(1, NSUB)))
+    for t, (lo, hi) in enumerate(parts):
+        if lo in cuts:
+            loads[cuts.index(lo)].wait()
         for b in range(8):
             p = place(b)
-            G[0, pl.ds(position(half_own, core, i), SUB), 128 * p:128 * p + 128] = (
-                g_f32[SUB * i:SUB * (i + 1), 128 * b:128 * b + 128].astype(BF16))
-        if i == 0:
+            G[0, pl.ds(pl.multiple_of(position(half_own, core, lo // SUB) + lo % SUB, FIRST), hi - lo), 128 * p:128 * p + 128] = (
+                g_f32[lo:hi, 128 * b:128 * b + 128].astype(BF16))
+        if t == 0:
             pl.semaphore_wait(barrier, 4)
         else:
-            send_own(i - 1)
-    loads[2].wait()
+            send_own(*parts[t - 1])
+    loads[-1].wait()
     for b in range(8):
         p = place(b)
         A0[:, 128 * p:128 * p + 128] = a_f32[:, 128 * b:128 * b + 128].astype(BF16)
-    send_own(NSUB - 1)
+    send_own(*parts[-1])
 
     def dot(a, g):
         return jnp.dot(a, g, preferred_element_type=F32)
@@ -333,7 +343,7 @@
                 pltpu.VMEM((ROWS, ORDER), F32),
                 pltpu.VMEM((ROWS, ORDER), F32),
                 pltpu.VMEM((3, 4, 1, ORDER), F32),
-                dma((3,)), dma((4,)), dma((3,)), dma((NSUB + 2,)),
+                dma((6,)), dma((4,)), dma((3,)), dma((NSUB + 2,)),
                 dma(()), dma(()), dma(()), dma(()), dma((NSUB,)),
                 dma(()), dma((len(PIECES_1) + len(PIECES_2) + 1,)),
             ],

time: 65.5 us -> 65 us (level)
  no operation moved by 1% of the time
where the time goes in v7:
time: 65 us; the launch traced here: 64.9 us
  Pallas kernels  64.9 us (100%)
    pallas_call x1, Pallas kernels, device_step(): pl.pallas_call(mcl_kernel, name='mcl', out_shape=(jax.ShapeDtypeStruct((R...  63.5 us
    pallas_call x1, Pallas kernels, device_step(): pl.pallas_call(scale_kernel, name='scale', out_shape=jax.ShapeDtypeStruct...  1.33 us

profile of v7, /device:TPU:0, one launch (start us, length us, event | category | flops | bytes accessed | tf_op | source)
XLA Modules:
  0.0 64.9 jit_solution(593347190919248766)
XLA Ops:
  0.0 63.5 %mcl.1 = (f32[512,1024]{1,0:T(8,128)S(1)}, f32[1,1024]{1,0:T(1,128)S(1)}) custom-call(f32[512,1024]{1,0:T(8,128)} %a_hbm.1, f32[512,1024]{1,0:T(8,128)} %g_hbm.1), custom_call_target="tpu_custom_call" | custom-call | tf_op jit(solution)/shard_map/mcl/pallas_call | solution.py:330
  63.6 1.3 %scale.1 = f32[512,1024]{1,0:T(8,128)} custom-call(f32[512,1024]{1,0:T(8,128)S(1)} %get-tuple-element.7.m_ref, f32[1,1024]{1,0:T(1,128)S(1)} %get-tuple-element.8.r_ref), custom_call_target="tpu_custom_call" | custom-call | tf_op jit(solution)/shard_map/scale/pallas_call | solution.py:352

commit v8 on v7

--- a/solution.py
+++ b/solution.py
@@ -58,7 +58,7 @@
         cp.start()
 
     barrier = pltpu.get_barrier_semaphore()
-    for dev in (nb_x, nb_y, nb_c, nb_xc):
+    for dev in (nb_x, nb_y, nb_c):
         pl.semaphore_signal(barrier, inc=1, device_id=dev, device_id_type=MESH)
 
     def rows(hc, half, side, sub, n=SUB):
@@ -118,7 +118,7 @@
             G[0, pl.ds(pl.multiple_of(position(half_own, core, lo // SUB) + lo % SUB, FIRST), hi - lo), 128 * p:128 * p + 128] = (
                 g_f32[lo:hi, 128 * b:128 * b + 128].astype(BF16))
         if t == 0:
-            pl.semaphore_wait(barrier, 4)
+            pl.semaphore_wait(barrier, 3)
         else:
             send_own(*parts[t - 1])
     loads[-1].wait()

time: 65 us -> 64.9 us (level)
  no operation moved by 1% of the time
where the time goes in v8:
time: 64.9 us; the launch traced here: 64.8 us
  Pallas kernels  64.8 us (100%)
    pallas_call x1, Pallas kernels, device_step(): pl.pallas_call(mcl_kernel, name='mcl', out_shape=(jax.ShapeDtypeStruct((R...  63.4 us
    pallas_call x1, Pallas kernels, device_step(): pl.pallas_call(scale_kernel, name='scale', out_shape=jax.ShapeDtypeStruct...  1.33 us

profile of v8, /device:TPU:0, one launch (start us, length us, event | category | flops | bytes accessed | tf_op | source)
XLA Modules:
  0.0 64.8 jit_solution(12621824015564379334)
XLA Ops:
  0.0 63.4 %mcl.1 = (f32[512,1024]{1,0:T(8,128)S(1)}, f32[1,1024]{1,0:T(1,128)S(1)}) custom-call(f32[512,1024]{1,0:T(8,128)} %a_hbm.1, f32[512,1024]{1,0:T(8,128)} %g_hbm.1), custom_call_target="tpu_custom_call" | custom-call | tf_op jit(solution)/shard_map/mcl/pallas_call | solution.py:330
  63.4 1.3 %scale.1 = f32[512,1024]{1,0:T(8,128)} custom-call(f32[512,1024]{1,0:T(8,128)S(1)} %get-tuple-element.7.m_ref, f32[1,1024]{1,0:T(1,128)S(1)} %get-tuple-element.8.r_ref), custom_call_target="tpu_custom_call" | custom-call | tf_op jit(solution)/shard_map/scale/pallas_call | solution.py:352

commit v9 on v8

--- a/solution.py
+++ b/solution.py
@@ -31,7 +31,7 @@
 
 
 def mcl_kernel(a_hbm, g_hbm, m_ref, r_ref,
-               a_f32, g_f32, G, A0, A1, A2, C1, C2, sums,
+               a_f32, g_f32, G, A0, A1, C1, C2, sums,
                ld_sem, snd, in_r, far_r, c0_r, c01_r, c2_r, c2x_r, c3_r, ar_s, ar_r):
     graph, col, row = lax.axis_index("graph"), lax.axis_index("col"), lax.axis_index("row")
     x, core = row // 2, row % 2
@@ -50,7 +50,7 @@
         return pltpu.make_async_remote_copy(src_ref=ref_src, dst_ref=ref_dst, send_sem=send, recv_sem=recv,
                                             device_id=dev, device_id_type=MESH)
 
-    cuts = (0, FIRST, 2 * FIRST, SUB, 2 * SUB, ROWS)
+    cuts = (0, FIRST, 2 * FIRST, SUB, ROWS)
     loads = [pltpu.make_async_copy(g_hbm.at[pl.ds(lo, hi - lo)], g_f32.at[pl.ds(lo, hi - lo)], ld_sem.at[i])
              for i, (lo, hi) in enumerate(zip(cuts, cuts[1:]))]
     loads.append(pltpu.make_async_copy(a_hbm, a_f32, ld_sem.at[len(loads)]))
@@ -87,7 +87,7 @@
     c2_cp = [remote(at, at, snd.at[1], c2_r, nb_c) for at in gy_at[:-1]]
     c2_cp += [remote(last_rows(1, half_own, e), last_rows(1, half_own, e), snd.at[3 if e else 1], c2x_r if e else c2_r, nb_c)
               for e in range(2)]
-    c3_cp = [remote(at, at, snd.at[0], c3_r.at[min(i, NSUB - 1)], nb_c) for i, at in enumerate(dx_at[:-1] + tail_d)]
+    c3_cp = [remote(at, at, snd.at[0], c3_r.at[0 if i < NSUB - 1 else 1], nb_c) for i, at in enumerate(dx_at[:-1] + tail_d)]
     ay_cp = [remote(A0.at[:, pl.ds(KC * n, KC)], A0.at[:, pl.ds(COLS + KC * n, KC)], snd.at[2], far_r.at[n if n < NKC - 1 else NSUB + 1], nb_y)
              for n in range(NKC)]
 
@@ -239,32 +239,25 @@
                         def _():
                             far_piece(NSUB)
 
-        bytes_of(SUB, snd.at[0], c3_r.at[n]).wait_recv()
+        if n < 2:
+            continue
+        bytes_of(SUB * (3 if n == 2 else 1), snd.at[0], c3_r.at[n - 2]).wait_recv()
         for first, width in PIECES_1:
             if first < COLS:
                 continue
-            d = dot(A0[:, lo:lo + KC], graph(lo, KC, first, width)) + dot(A0[:, hi:hi + KC], graph(hi, KC, first, width))
-            if n == 0:
-                C1[:, first:first + width] = d
-            elif n < NKC - 1:
-                C1[:, first:first + width] += d
+            if n == 2:
+                C1[:, first:first + width] = (dot(A0[:, :hi - COLS + KC], graph(0, lo + KC, first, width))
+                                              + dot(A0[:, COLS:hi + KC], graph(COLS, lo + KC, first, width)))
             else:
+                d = dot(A0[:, lo:lo + KC], graph(lo, KC, first, width)) + dot(A0[:, hi:hi + KC], graph(hi, KC, first, width))
                 shared.append(square_and_share(0, C1, first, width, C1[:, first:first + width] + d))
 
     bytes_of(2 * ROWS, snd.at[2], c2_r).wait_send()
     bytes_of(ROWS, snd.at[0], c2_r).wait_send()
-    done = 0
-    for t in range(1):
-        rescale(A1, C1, shared[t])
-        lo, depth = PIECES_1[t]
-        for hc in range(2):
-            at = slice(hc * COLS, (hc + 1) * COLS)
-            d = dot(A1[:, lo:lo + depth], G[hc, lo:lo + depth, :])
-            if t == 0:
-                C2[:, at] = d
-            else:
-                C2[:, at] += d
-        done = lo + depth
+    lo, depth = PIECES_1[0]
+    a = (C1[:, lo:lo + depth] * gathered(shared[0])).astype(BF16)
+    for hc in range(2):
+        C2[:, hc * COLS:(hc + 1) * COLS] = dot(a, G[hc, lo:lo + depth, :])
     rescale(A1, C1, shared[1])
     lo, depth = PIECES_1[1]
     for first, width in PIECES_2[:EARLY]:
@@ -289,10 +282,10 @@
     shared.append(share(1, *held))
 
     for t, (lo, depth) in enumerate(PIECES_2):
-        rescale(A2, C2, shared[t])
+        f = gathered(shared[t])
         if t == len(PIECES_2) - 1:
             three(1, 0, ORDER, 0).wait_send()
-        d = dot(A2[:, lo:lo + depth], G[0, lo:lo + depth, :])
+        d = dot((C2[:, lo:lo + depth] * f).astype(BF16), G[0, lo:lo + depth, :])
         if t == 0:
             C1[:, :COLS] = d
         elif t < len(PIECES_2) - 1:
@@ -339,12 +332,11 @@
                 pltpu.VMEM((2, ORDER, COLS), BF16),
                 pltpu.VMEM((ROWS, ORDER), BF16),
                 pltpu.VMEM((ROWS, ORDER), BF16),
-                pltpu.VMEM((ROWS, ORDER), BF16),
                 pltpu.VMEM((ROWS, ORDER), F32),
                 pltpu.VMEM((ROWS, ORDER), F32),
                 pltpu.VMEM((3, 4, 1, ORDER), F32),
-                dma((6,)), dma((4,)), dma((3,)), dma((NSUB + 2,)),
-                dma(()), dma(()), dma(()), dma(()), dma((NSUB,)),
+                dma((5,)), dma((4,)), dma((3,)), dma((NSUB + 2,)),
+                dma(()), dma(()), dma(()), dma(()), dma((2,)),
                 dma(()), dma((len(PIECES_1) + len(PIECES_2) + 1,)),
             ],
             compiler_params=pltpu.CompilerParams(collective_id=0, has_side_effects=True, vmem_limit_bytes=48 * 2**20),

time: 64.9 us -> 64.8 us (level)
  no operation moved by 1% of the time
where the time goes in v9:
time: 64.8 us; the launch traced here: 64.7 us
  Pallas kernels  64.7 us (100%)
    pallas_call x1, Pallas kernels, device_step(): pl.pallas_call(mcl_kernel, name='mcl', out_shape=(jax.ShapeDtypeStruct((R...  63.3 us
    pallas_call x1, Pallas kernels, device_step(): pl.pallas_call(scale_kernel, name='scale', out_shape=jax.ShapeDtypeStruct...  1.33 us

profile of v9, /device:TPU:0, one launch (start us, length us, event | category | flops | bytes accessed | tf_op | source)
XLA Modules:
  0.0 64.7 jit_solution(1781724478811097109)
XLA Ops:
  0.0 63.3 %mcl.1 = (f32[512,1024]{1,0:T(8,128)S(1)}, f32[1,1024]{1,0:T(1,128)S(1)}) custom-call(f32[512,1024]{1,0:T(8,128)} %a_hbm.1, f32[512,1024]{1,0:T(8,128)} %g_hbm.1), custom_call_target="tpu_custom_call" | custom-call | tf_op jit(solution)/shard_map/mcl/pallas_call | solution.py:323
  63.3 1.3 %scale.1 = f32[512,1024]{1,0:T(8,128)} custom-call(f32[512,1024]{1,0:T(8,128)S(1)} %get-tuple-element.7.m_ref, f32[1,1024]{1,0:T(1,128)S(1)} %get-tuple-element.8.r_ref), custom_call_target="tpu_custom_call" | custom-call | tf_op jit(solution)/shard_map/scale/pallas_call | solution.py:344

commit v10 on v9

--- a/solution.py
+++ b/solution.py
@@ -50,7 +50,7 @@
         return pltpu.make_async_remote_copy(src_ref=ref_src, dst_ref=ref_dst, send_sem=send, recv_sem=recv,
                                             device_id=dev, device_id_type=MESH)
 
-    cuts = (0, FIRST, 2 * FIRST, SUB, ROWS)
+    cuts = (0, FIRST, 2 * FIRST, ROWS)
     loads = [pltpu.make_async_copy(g_hbm.at[pl.ds(lo, hi - lo)], g_f32.at[pl.ds(lo, hi - lo)], ld_sem.at[i])
              for i, (lo, hi) in enumerate(zip(cuts, cuts[1:]))]
     loads.append(pltpu.make_async_copy(a_hbm, a_f32, ld_sem.at[len(loads)]))
@@ -109,7 +109,7 @@
             remote(at, there, snd.at[0], in_r.at[0], nb_y).start()
             remote(at, at, snd.at[0], c01_r, nb_c).start()
 
-    parts = (*zip(cuts, cuts[1:4]), *((SUB * i, SUB * (i + 1)) for i in range(1, NSUB)))
+    parts = (*zip((0, FIRST, 2 * FIRST), (FIRST, 2 * FIRST, SUB)), *((SUB * i, SUB * (i + 1)) for i in range(1, NSUB)))
     for t, (lo, hi) in enumerate(parts):
         if lo in cuts:
             loads[cuts.index(lo)].wait()
@@ -306,8 +306,8 @@
 
 def scale_kernel(m_ref, r_ref, out_hbm, out, sem):
     factor = r_ref[...]
-    step = ROWS // 8
-    for i in range(8):
+    step = ROWS // 16
+    for i in range(16):
         at = pl.ds(step * i, step)
         out[at, :] = m_ref[at, :] * factor
         pltpu.make_async_copy(out.at[at], out_hbm.at[at], sem).start()
@@ -335,7 +335,7 @@
                 pltpu.VMEM((ROWS, ORDER), F32),
                 pltpu.VMEM((ROWS, ORDER), F32),
                 pltpu.VMEM((3, 4, 1, ORDER), F32),
-                dma((5,)), dma((4,)), dma((3,)), dma((NSUB + 2,)),
+                dma((4,)), dma((4,)), dma((3,)), dma((NSUB + 2,)),
                 dma(()), dma(()), dma(()), dma(()), dma((2,)),
                 dma(()), dma((len(PIECES_1) + len(PIECES_2) + 1,)),
             ],

time: 64.8 us -> 64.7 us (level)
  no operation moved by 1% of the time
where the time goes in v10:
time: 64.7 us
  Pallas kernels  64.6 us (100%)
    pallas_call x1, Pallas kernels, device_step(): pl.pallas_call(mcl_kernel, name='mcl', out_shape=(jax.ShapeDtypeStruct((R...  63.3 us
    pallas_call x1, Pallas kernels, device_step(): pl.pallas_call(scale_kernel, name='scale', out_shape=jax.ShapeDtypeStruct...  1.32 us

profile of v10, /device:TPU:0, one launch (start us, length us, event | category | flops | bytes accessed | tf_op | source)
XLA Modules:
  0.0 64.7 jit_solution(11738818605962032171)
XLA Ops:
  0.0 63.3 %mcl.1 = (f32[512,1024]{1,0:T(8,128)S(1)}, f32[1,1024]{1,0:T(1,128)S(1)}) custom-call(f32[512,1024]{1,0:T(8,128)} %a_hbm.1, f32[512,1024]{1,0:T(8,128)} %g_hbm.1), custom_call_target="tpu_custom_call" | custom-call | tf_op jit(solution)/shard_map/mcl/pallas_call | solution.py:323
  63.3 1.3 %scale.1 = f32[512,1024]{1,0:T(8,128)} custom-call(f32[512,1024]{1,0:T(8,128)S(1)} %get-tuple-element.7.m_ref, f32[1,1024]{1,0:T(1,128)S(1)} %get-tuple-element.8.r_ref), custom_call_target="tpu_custom_call" | custom-call | tf_op jit(solution)/shard_map/scale/pallas_call | solution.py:344

commit v11 on v10

--- a/solution.py
+++ b/solution.py
@@ -282,9 +282,9 @@
     shared.append(share(1, *held))
 
     for t, (lo, depth) in enumerate(PIECES_2):
-        f = gathered(shared[t])
         if t == len(PIECES_2) - 1:
             three(1, 0, ORDER, 0).wait_send()
+        f = gathered(shared[t])
         d = dot((C2[:, lo:lo + depth] * f).astype(BF16), G[0, lo:lo + depth, :])
         if t == 0:
             C1[:, :COLS] = d

time: 64.7 us -> 64.7 us (level)
  no operation moved by 1% of the time
where the time goes in v11:
time: 64.7 us; the launch traced here: 64.6 us
  Pallas kernels  64.6 us (100%)
    pallas_call x1, Pallas kernels, device_step(): pl.pallas_call(mcl_kernel, name='mcl', out_shape=(jax.ShapeDtypeStruct((R...  63.3 us
    pallas_call x1, Pallas kernels, device_step(): pl.pallas_call(scale_kernel, name='scale', out_shape=jax.ShapeDtypeStruct...  1.32 us

profile of v11, /device:TPU:0, one launch (start us, length us, event | category | flops | bytes accessed | tf_op | source)
XLA Modules:
  0.0 64.6 jit_solution(17294173411729545737)
XLA Ops:
  0.0 63.3 %mcl.1 = (f32[512,1024]{1,0:T(8,128)S(1)}, f32[1,1024]{1,0:T(1,128)S(1)}) custom-call(f32[512,1024]{1,0:T(8,128)} %a_hbm.1, f32[512,1024]{1,0:T(8,128)} %g_hbm.1), custom_call_target="tpu_custom_call" | custom-call | tf_op jit(solution)/shard_map/mcl/pallas_call | solution.py:323
  63.3 1.3 %scale.1 = f32[512,1024]{1,0:T(8,128)} custom-call(f32[512,1024]{1,0:T(8,128)S(1)} %get-tuple-element.7.m_ref, f32[1,1024]{1,0:T(1,128)S(1)} %get-tuple-element.8.r_ref), custom_call_target="tpu_custom_call" | custom-call | tf_op jit(solution)/shard_map/scale/pallas_call | solution.py:344

commit v12 on v11

--- a/solution.py
+++ b/solution.py
@@ -21,7 +21,7 @@
 KC = 256
 NKC = COLS // KC
 PIECES_1 = ((0, 512), (512, 512), (1024, 1024))
-EARLY = 2
+EARLY = 1
 STEP = 512
 PIECES_2 = ((1024, 512), (1536, 512), (0, 512), (512, 512))
 

time: 64.7 us -> 64.7 us (level)
  no operation moved by 1% of the time
where the time goes in v12:
time: 64.7 us; the launch traced here: 64.6 us
  Pallas kernels  64.6 us (100%)
    pallas_call x1, Pallas kernels, device_step(): pl.pallas_call(mcl_kernel, name='mcl', out_shape=(jax.ShapeDtypeStruct((R...  63.3 us
    pallas_call x1, Pallas kernels, device_step(): pl.pallas_call(scale_kernel, name='scale', out_shape=jax.ShapeDtypeStruct...  1.32 us

profile of v12, /device:TPU:0, one launch (start us, length us, event | category | flops | bytes accessed | tf_op | source)
XLA Modules:
  0.0 64.6 jit_solution(9112958781497905337)
XLA Ops:
  0.0 63.3 %mcl.1 = (f32[512,1024]{1,0:T(8,128)S(1)}, f32[1,1024]{1,0:T(1,128)S(1)}) custom-call(f32[512,1024]{1,0:T(8,128)} %a_hbm.1, f32[512,1024]{1,0:T(8,128)} %g_hbm.1), custom_call_target="tpu_custom_call" | custom-call | tf_op jit(solution)/shard_map/mcl/pallas_call | solution.py:323
  63.3 1.3 %scale.1 = f32[512,1024]{1,0:T(8,128)} custom-call(f32[512,1024]{1,0:T(8,128)S(1)} %get-tuple-element.7.m_ref, f32[1,1024]{1,0:T(1,128)S(1)} %get-tuple-element.8.r_ref), custom_call_target="tpu_custom_call" | custom-call | tf_op jit(solution)/shard_map/scale/pallas_call | solution.py:344
